TPU v7x, 128 devices: a whole 4x4x4 slice. The times are simulated.
128 devices in a mesh: zero: 32 (over z, x, core), model: 4 (over y).
Axes of the slice: x: 4, y: 4, z: 4, core: 2. Of those that a mesh axis runs over, the one named last changes fastest.
Arguments:
- w_query: bfloat16 [4096, 4096], P('zero', 'model'), may hold values from -0.1875 to 0.1875
- low_query: bfloat16 [4096, 16], P('zero'), may hold values from -0.09375 to 0.09375
- high_query: bfloat16 [16, 4096], P(None, 'model'), may hold values from -1.5 to 1.5
- w_key: bfloat16 [4096, 4096], P('zero', 'model'), may hold values from -0.1875 to 0.1875
- low_key: bfloat16 [4096, 16], P('zero'), may hold values from -0.09375 to 0.09375
- high_key: bfloat16 [16, 4096], P(None, 'model'), may hold values from -1.5 to 1.5
- w_value: bfloat16 [4096, 4096], P('zero', 'model'), may hold values from -0.1875 to 0.1875
- low_value: bfloat16 [4096, 16], P('zero'), may hold values from -0.09375 to 0.09375
- high_value: bfloat16 [16, 4096], P(None, 'model'), may hold values from -1.5 to 1.5
- norm_train: float32 [4096], P(('zero', 'model')), may hold values from 0.25 to 1.75
- norm_step: float32 [4096], P(('zero', 'model')), may hold values from -0.3 to 0.3
Outputs:
- serving_query: bfloat16 [4096, 4096], P(None, 'model')
- serving_key: bfloat16 [4096, 4096], P(None, 'model')
- serving_value: bfloat16 [4096, 4096], P(None, 'model')
- factor_query: float32 [4096], P('model')
- factor_key: float32 [4096], P('model')
- factor_value: float32 [4096], P('model')
- serve_norm: bfloat16 [4096], replicated
All inputs are finite; a program needn't handle non-finite values. Where the computation divides by a largest or mean magnitude, that divisor is 1e-20 or more.
Results may differ from a plain program's by a relative error of at most 0.001.
Values may be sent and summed in bfloat16 or wider, within the bound.
A program may use at most 128 MiB of HBM per device.

v0:
```python
import jax
import jax.numpy as jnp
from jax import lax
from jax.sharding import Mesh
from jax.sharding import PartitionSpec as P

D_MODEL = 4096
ZERO = ("zero_0", "zero_1", "zero_2")
ZERO_MODEL = ("zero_0", "zero_1", "zero_2", "model")


mix_rate = 0.5


def copy_for_each(x, axis):
    copies = jnp.broadcast_to(x, (lax.axis_size(axis), *x.shape))
    return lax.all_to_all(copies, axis, split_axis=0, concat_axis=0, tiled=True)


def taken_together(x, axis):
    return copy_for_each(x, axis).sum(axis=0)


def together(arrays, axis):
    vector, at, done = (jnp.concatenate([a.reshape(-1) for a in arrays]), 0, [])
    so_far = taken_together(vector, axis)
    for a in arrays:
        done.append(so_far[at : at + a.size].reshape(a.shape))
        at += a.size
    return tuple(done)


def sent_together(arrays, axis, dim, along):
    widths = [a.shape[along] for a in arrays]
    both = jnp.concatenate(arrays, axis=along)
    out = lax.all_gather(both, axis, axis=dim, tiled=True)
    return tuple(jnp.split(out, [sum(widths[:k]) for k in range(1, len(widths))], axis=along))


def laid_out(tiles, dim):
    dims = list(tiles.shape[1:])
    dims[dim] *= tiles.shape[0]
    return jnp.moveaxis(tiles, 0, dim).reshape(dims)


def gather_in_order(x, axes, turns):
    tiles = x
    for k in turns:
        tiles = lax.all_gather(tiles, axes[k])
    done = turns[::-1]
    back = [done.index(k) for k in range(len(axes))]
    tiles = tiles.transpose(*back, *range(len(axes), tiles.ndim))
    return tiles.reshape(-1, *x.shape)


def gather_axes(x, axes, turns, dim):
    return laid_out(gather_in_order(x, axes, turns), dim)


def per_device(
    w_query,
    low_query,
    high_query,
    w_key,
    low_key,
    high_key,
    w_value,
    low_value,
    high_value,
    norm_train,
    norm_step,
):
    whole_query = w_query.astype(jnp.float32) + mix_rate * jnp.dot(
        low_query, high_query, preferred_element_type=jnp.float32
    )
    whole_key = w_key.astype(jnp.float32) + mix_rate * jnp.dot(
        low_key, high_key, preferred_element_type=jnp.float32
    )
    whole_value = w_value.astype(jnp.float32) + mix_rate * jnp.dot(
        low_value, high_value, preferred_element_type=jnp.float32
    )
    total_query, total_key, total_value = together(
        (
            jnp.sum(jnp.abs(whole_query), axis=0),
            jnp.sum(jnp.abs(whole_key), axis=0),
            jnp.sum(jnp.abs(whole_value), axis=0),
        ),
        ZERO,
    )
    factor_query = total_query / D_MODEL
    factor_key = total_key / D_MODEL
    factor_value = total_value / D_MODEL
    narrow_query, narrow_key, narrow_value = (
        (whole_query / factor_query).astype(jnp.bfloat16),
        (whole_key / factor_key).astype(jnp.bfloat16),
        (whole_value / factor_value).astype(jnp.bfloat16),
    )
    serving_query, serving_key, serving_value = sent_together(
        (narrow_query, narrow_key, narrow_value), ZERO, 0, 1
    )
    serve_norm = gather_axes(
        (norm_train + norm_step).astype(jnp.bfloat16), ZERO_MODEL, (0, 1, 3, 2), 0
    )
    return (
        serving_query,
        serving_key,
        serving_value,
        factor_query,
        factor_key,
        factor_value,
        serve_norm,
    )


def solution(mesh):
    torus = Mesh(
        mesh.devices.reshape(4, 4, 2, mesh.shape["model"]), ("zero_0", "zero_1", "zero_2", "model")
    )
    in_specs = (
        P(ZERO, "model"),
        P(ZERO, None),
        P(None, "model"),
        P(ZERO, "model"),
        P(ZERO, None),
        P(None, "model"),
        P(ZERO, "model"),
        P(ZERO, None),
        P(None, "model"),
        P(ZERO_MODEL),
        P(ZERO_MODEL),
    )
    out_specs = (
        P(None, "model"),
        P(None, "model"),
        P(None, "model"),
        P("model"),
        P("model"),
        P("model"),
        P(),
    )
    return jax.shard_map(
        per_device, mesh=torus, in_specs=in_specs, out_specs=out_specs, check_vma=False
    )
```

profile of v0, /device:TPU:1, one launch (start us, length us, event | category | flops | bytes accessed | tf_op | source)
XLA Modules:
  0.0 146.7 jit_solution(5379046521932626745)
XLA Ops:
  7.2 0.0 copy-start
  7.2 0.0 copy-start.6
  7.2 0.0 copy-start.4
  7.2 0.0 copy-start.5
  7.2 0.0 all-gather.7.cloned.1.call-start
  7.3 0.7 copy-done
  7.9 1.2 abs_reduce_fusion
  9.2 1.3 abs_reduce_fusion.1
  10.4 1.3 abs_reduce_fusion.2
  11.7 0.2 broadcast_in_dim.2
  11.9 19.4 %all_to_all.6 = f32[32,1,3072]{2,1,0:T(1,128)S(1)} all-to-all(f32[32,1,3072]{2,1,0:T(1,128)S(1)} %broadcast_in_dim.2), channel_id=1, replica_groups=mesh['zero_0'=4,'zero_1'=4,'zero_2'=2,'model'=4] {'zero_0','zero_1','zer..., dimensions={0} | all-to-all | bytes 786432 | tf_op jit(solution)/shard_map/all_to_all | solution.py:17
  31.3 0.2 reduce_sum.39
  31.6 0.0 copy-start.1
  31.6 0.0 copy-start.2
  31.6 0.0 copy-start.3
  31.6 0.1 divide_convert_fusion
  31.8 0.9 pad_maximum_fusion
  32.7 0.0 all-gather.7.cloned.1.call-update
  32.7 0.0 copy-done.6
  32.7 0.6 dynamic-slice
  34.0 0.0 copy-done.4
  34.0 0.0 copy-done.5
  34.0 0.2 dynamic-update-slice
  34.3 6.8 %all-reduce = bf16[128]{0:T(256)(128)(2,1)S(1)} all-reduce(bf16[128]{0:T(256)(128)(2,1)S(1)} %dynamic-update-slice), channel_id=2, replica_groups=mesh['zero_0'=4,'zero_1'=4,'zero_2'=2,'model'=4] {'zero_0'}, use_global_device_ids=true, to_apply=%add | all-reduce | flops 128 | bytes 512
  41.1 0.1 reshape.28
  41.2 7.9 %all-gather.4 = bf16[4,4,32]{2,1,0:T(4,128)(2,1)S(1)} all-gather(bf16[1,4,32]{2,1,0:T(4,128)(2,1)S(1)} %reshape.28), channel_id=3, replica_groups=mesh['zero_0'=4,'zero_1'=4,'zero_2'=2,'model'=4] {'zero_1'}, dimensions={0}, use_global_device_ids=true | all-gather | bytes 1280 | tf_op jit(solution)/shard_map/all_gather | solution.py:49
  49.1 10.3 %all-gather.2 = bf16[16,4,32]{2,1,0:T(4,128)(2,1)S(1)} all-gather(bf16[4,4,32]{2,1,0:T(4,128)(2,1)S(1)} %all-gather.4), channel_id=4, replica_groups=mesh['zero_0'=4,'zero_1'=4,'zero_2'=2,'model'=4] {'model'}, dimensions={0}, use_global_device_ids=true | all-gather | bytes 5120 | tf_op jit(solution)/shard_map/all_gather | solution.py:49
  59.4 6.0 %all-gather.3 = bf16[8,4,4,32]{3,2,1,0:T(4,128)(2,1)S(1)} all-gather(bf16[4,4,4,32]{3,2,1,0:T(4,128)(2,1)S(1)} %bitcast.14), channel_id=5, replica_groups=mesh['zero_0'=4,'zero_1'=4,'zero_2'=2,'model'=4] {'zero_2'}, dimensions={0}, use_global_device_ids=true | all-gather | bytes 12288 | tf_op jit(solution)/shard_map/all_gather | solution.py:49
  65.4 0.7 reshape_reshape.3
  66.1 56.7 %all-gather.7.cloned.1.call-done = bf16[4096,3072]{1,0:T(8,128)(2,1)} async-done(((bf16[128,3072]{1,0:T(8,128)(2,1)}), bf16[4096,3072]{1,0:T(8,128)(2,1)}) %all-gather.7.cloned.1.call-update) | async-done | bytes 25165840 | tf_op jit(solution)/shard_map/all_gather | solution.py:36
  122.8 17.0 %fusion.3 = (bf16[4096,1024]{1,0:T(8,128)(2,1)}, bf16[4096,1024]{1,0:T(8,128)(2,1)}, bf16[4096,1024]{1,0:T(8,128)(2,1)}) fusion(bf16[4096,3072]{1,0:T(8,128)(2,1)} %all-gather.7.cloned.1.call-done), kind=kLoop, calls=%fused_computation.19 | loop fusion | bytes 50331648 | tf_op jit(solution)/shard_map/split | solution.py:37
  139.8 0.0 copy-done.1
  139.8 0.0 copy-done.2
  139.8 0.0 copy-done.3
  (6 shorter events, 0.1 us)
Async XLA Ops:
  7.2 0.8 copy-start
  7.2 25.5 %copy-start.6 = (u32[128]{0:T(128)S(1)}, u32[128]{0:T(128)}, u32[]{:S(2)}) copy-start(u32[128]{0:T(128)} %constant.13) | copy-start | bytes 1540
  7.2 26.8 %copy-start.4 = (f32[32]{0:T(128)S(1)}, f32[32]{0:T(128)}, u32[]{:S(2)}) copy-start(f32[32]{0:T(128)} %param.20) | copy-start | bytes 388
  7.2 26.8 %copy-start.5 = (f32[32]{0:T(128)S(1)}, f32[32]{0:T(128)}, u32[]{:S(2)}) copy-start(f32[32]{0:T(128)} %param.21) | copy-start | bytes 388
  7.2 115.6 %all-gather.7.cloned.1.call-start = ((), (), s32[]{:S(2)}) async-start(), calls=%async_computation.1 | async-start | bytes 25952256 | tf_op jit(solution)/shard_map/all_gather | solution.py:36
  31.6 108.3 %copy-start.1 = (f32[1024]{0:T(1024)}, f32[1024]{0:T(1024)S(1)}, u32[]{:S(2)}) copy-start(f32[1024]{0:T(1024)S(1)} %get-tuple-element.10) | copy-start | bytes 12292
  31.6 108.3 %copy-start.2 = (f32[1024]{0:T(1024)}, f32[1024]{0:T(1024)S(1)}, u32[]{:S(2)}) copy-start(f32[1024]{0:T(1024)S(1)} %get-tuple-element.11) | copy-start | bytes 12292
  31.6 108.3 %copy-start.3 = (f32[1024]{0:T(1024)}, f32[1024]{0:T(1024)S(1)}, u32[]{:S(2)}) copy-start(f32[1024]{0:T(1024)S(1)} %get-tuple-element.12) | copy-start | bytes 12292
Sparse Core Ops, SparseCore 0:
  32.8 89.9 all-gather.6
where the time goes:
time: 147 us
  waiting for transfers between devices  56.7 us (39%)
  blocking collectives  50.4 us (34%)
  local copies, waits for them, and re-layouts  19.5 us (13%)
  between operations  14.9 us (10%)
  matrix products  3.76 us (3%)
    all_gather x1, waiting for transfers between devices, sent_together(): out = lax.all_gather(both, axis, axis=dim, tiled=True)  56.7 us
    all_gather x3, blocking collectives, gather_in_order(): tiles = lax.all_gather(tiles, axes[k])  24.2 us
    all_to_all x1, blocking collectives, copy_for_each(): return lax.all_to_all(copies, axis, split_axis=0, concat_axis=0, tiled=True)  19.4 us
    split x1, local copies, waits for them, and re-layouts, sent_together(): jnp.split(out, [sum(widths[:k]) for k in range(1, len(widths))], axis=along)  17 us
    unnamed x1, blocking collectives  6.84 us
  transfers between devices with their start and end apart: 1, of which 1 were waited for; matrix products, arithmetic and copies ran while one was open for 1% of the time, Pallas kernels for 0%

commit v1 on v0

v1 whole, which is shorter than its diff:
```python
import jax
import jax.numpy as jnp
from jax import lax
from jax.experimental import pallas as pl
from jax.experimental.pallas import tpu as pltpu
from jax.sharding import PartitionSpec as P

MESH = pl.DeviceIdType.MESH
D_MODEL = 4096
COLS = 1024
ROWS = 128
SUB = 32
SIDE = 4
AHEAD = 4

SLOTS = (
    (0, 0, 0, 0),
    (0, 0, 0, 1),
    (0, 0, 1, 0),
    (0, 0, 1, 1),
    (-1, 0, 0, 0),
    (0, -1, 1, 0),
    (0, 1, 1, 0),
    (0, -1, 1, 1),
    (0, 1, 1, 1),
    (0, 2, 1, 0),
    (0, 2, 1, 1),
    (-1, 0, 1, 0),
    (-1, -1, 1, 0),
    (-1, 1, 1, 0),
    (-1, 2, 1, 0),
)
N_SLOTS = len(SLOTS)


def gather_kernel(
    w_query, w_key, w_value, low_query, low_key, low_value, high_query, high_key, high_value, train, step,
    factors, norm, full,
    weights, lows, highs, whole, message, from_y, from_core, from_x, from_z,
    load_sem, small_send, small_recv, send_sem, recv_sem, pass_send, pass_recv, own_send, own_recv,
):
    zero, y = lax.axis_index("zero"), lax.axis_index("model")
    z, x, core = zero // 8, zero // 2 % 4, zero % 2
    partner = zero + 1 - 2 * core

    def index_of(z_at, x_at):
        return (z_at * 4 + x_at) * 2 + core

    loads = [
        pltpu.make_async_copy(src, dst, load_sem.at[k])
        for k, (src, dst) in enumerate(
            (
                (low_query, lows.at[0]), (low_key, lows.at[1]), (low_value, lows.at[2]),
                (high_query, highs.at[0]), (high_key, highs.at[1]), (high_value, highs.at[2]),
                (w_query, weights.at[0]), (w_key, weights.at[1]), (w_value, weights.at[2]),
            )
        )
    ]
    for load in loads:
        load.start()

    barrier = pltpu.get_barrier_semaphore()
    pl.semaphore_signal(barrier, inc=1, device_id=(partner, y), device_id_type=MESH)
    for k in range(1, SIDE):
        pl.semaphore_signal(barrier, inc=1, device_id=(index_of(z, (x + k) % 4), y), device_id_type=MESH)
        pl.semaphore_signal(barrier, inc=1, device_id=(index_of((z + k) % 4, x), y), device_id_type=MESH)
        pl.semaphore_signal(barrier, inc=1, device_id=(zero, (y + k) % 4), device_id_type=MESH)

    gain = train[...] + step[...]
    gain = pltpu.roll(jnp.concatenate([gain, jnp.zeros((1, 96), jnp.float32)], axis=1), 32 * y, 1)
    row = lax.broadcasted_iota(jnp.int32, (8, 128), 0)
    tile = jnp.where(row == x * 2 + core, jnp.broadcast_to(gain, (8, 128)), 0.0)
    from_y[pl.ds(y, 1)] = tile[None]
    pl.semaphore_wait(barrier, 10)

    def y_copy(k):
        return pltpu.make_async_remote_copy(
            src_ref=from_y.at[y], dst_ref=from_y.at[y],
            send_sem=small_send.at[k], recv_sem=small_recv.at[k],
            device_id=(zero, (y + k) % 4), device_id_type=MESH,
        )

    for k in range(1, SIDE):
        y_copy(k).start()

    for load in loads:
        load.wait()
    for m in range(3):
        product = lax.dot_general(
            lows[m], highs[m], (((0,), (0,)), ((), ())), preferred_element_type=jnp.float32
        )
        value = weights[m].astype(jnp.float32) + 0.5 * product
        whole[m] = value
        total = jnp.sum(jnp.abs(value), axis=0, keepdims=True)
        for j in range(8):
            message[m * 8 + j : m * 8 + j + 1, :] = total[:, j * 128 : (j + 1) * 128]
    for k in range(1, SIDE):
        y_copy(k).wait()
    message[24:32, :] = from_y[0] + from_y[1] + from_y[2] + from_y[3]

    core_copy = pltpu.make_async_remote_copy(
        src_ref=message, dst_ref=from_core,
        send_sem=small_send.at[0], recv_sem=small_recv.at[0],
        device_id=(partner, y), device_id_type=MESH,
    )
    core_copy.start()
    core_copy.wait()
    from_x[pl.ds(x, 1)] = (message[...] + from_core[...])[None]

    def x_copy(k):
        return pltpu.make_async_remote_copy(
            src_ref=from_x.at[x], dst_ref=from_x.at[x],
            send_sem=small_send.at[3 + k], recv_sem=small_recv.at[3 + k],
            device_id=(index_of(z, (x + k) % 4), y), device_id_type=MESH,
        )

    for k in range(1, SIDE):
        x_copy(k).start()
    for k in range(1, SIDE):
        x_copy(k).wait()
    from_z[pl.ds(z, 1)] = (from_x[0] + from_x[1] + from_x[2] + from_x[3])[None]

    def z_copy(k):
        return pltpu.make_async_remote_copy(
            src_ref=from_z.at[z], dst_ref=from_z.at[z],
            send_sem=small_send.at[6 + k], recv_sem=small_recv.at[6 + k],
            device_id=(index_of((z + k) % 4, x), y), device_id_type=MESH,
        )

    for k in range(1, SIDE):
        z_copy(k).start()
    for k in range(1, SIDE):
        z_copy(k).wait()
    total = from_z[0] + from_z[1] + from_z[2] + from_z[3]
    factor = total[:24] / D_MODEL
    factors[...] = factor
    inverse = 1.0 / factor
    for k in range(SIDE):
        norm[k * 8 : (k + 1) * 8, :] = from_z[k, 24:32, :].astype(jnp.bfloat16)

    own = pl.multiple_of(zero * ROWS, ROWS)
    for m in range(3):
        for j in range(8):
            scale = inverse[m * 8 + j : m * 8 + j + 1, :]
            full[m, pl.ds(own, ROWS), j * 128 : (j + 1) * 128] = (
                whole[m, :, j * 128 : (j + 1) * 128] * scale
            ).astype(jnp.bfloat16)

    def rows_of(link, slot, arriving):
        along, across, half, part = SLOTS[slot]
        axis, way = link // 2, 1 - 2 * (link % 2)
        along = (along - arriving) * way
        z_at = (z + axis * along + (1 - axis) * across + 8) % 4
        x_at = (x + (1 - axis) * along + axis * across + 8) % 4
        half = axis if half == 0 else 1 - axis
        part = link % 2 if part == 0 else 1 - link % 2
        return pl.multiple_of(index_of(z_at, x_at) * ROWS + half * 64 + part * SUB, SUB)

    def link_copy(link, slot, arriving=0):
        axis, way = link // 2, 1 - 2 * (link % 2)
        target = index_of((z + axis * way + 4) % 4, (x + (1 - axis) * way + 4) % 4)
        chunk = full.at[:, pl.ds(rows_of(link, slot, arriving), SUB), :]
        return pltpu.make_async_remote_copy(
            src_ref=chunk, dst_ref=chunk,
            send_sem=send_sem.at[slot * 4 + link], recv_sem=recv_sem.at[slot * 4 + link],
            device_id=(target, y), device_id_type=MESH,
        )

    def pass_copy(link, slot):
        chunk = full.at[:, pl.ds(rows_of(link, slot, 1), SUB), :]
        return pltpu.make_async_remote_copy(
            src_ref=chunk, dst_ref=chunk,
            send_sem=pass_send.at[slot * 4 + link], recv_sem=pass_recv.at[slot * 4 + link],
            device_id=(partner, y), device_id_type=MESH,
        )

    def each_link(body):
        def step_of(link, carry):
            body(link)
            return carry

        lax.fori_loop(0, 4, step_of, 0)

    for slot in range(AHEAD):
        each_link(lambda link: link_copy(link, slot).start())
    block = full.at[:, pl.ds(own, ROWS), :]
    own_copy = pltpu.make_async_remote_copy(
        src_ref=block, dst_ref=block, send_sem=own_send, recv_sem=own_recv,
        device_id=(partner, y), device_id_type=MESH,
    )
    own_copy.start()

    for slot in range(N_SLOTS):

        def arrive(link):
            link_copy(link, slot, 1).wait_recv()
            pass_copy(link, slot).start()

        each_link(arrive)
        if slot + AHEAD < N_SLOTS:
            each_link(lambda link: link_copy(link, slot + AHEAD).start())

    for slot in range(N_SLOTS):

        def finish(link):
            link_copy(link, slot).wait_send()
            pass_copy(link, slot).wait()

        each_link(finish)
    own_copy.wait()


def write_kernel(factors, norm, full, query, key, value, f_query, f_key, f_value, norm_out, sem):
    cuts = 4
    step = D_MODEL // cuts
    copies = [
        pltpu.make_async_copy(
            full.at[m, pl.ds(c * step, step), :], out.at[pl.ds(c * step, step), :], sem.at[m * cuts + c]
        )
        for m, out in enumerate((query, key, value))
        for c in range(cuts)
    ]
    for copy in copies:
        copy.start()
    for m, out in enumerate((f_query, f_key, f_value)):
        out[...] = factors[m * 8 : (m + 1) * 8, :]
    norm_out[...] = norm[...]
    for copy in copies:
        copy.wait()


def per_device(wq, lq, hq, wk, lk, hk, wv, lv, hv, train, step):
    any_spec = pl.BlockSpec(memory_space=pl.ANY)
    vmem = pl.BlockSpec(memory_space=pltpu.VMEM)
    f32, bf16 = jnp.float32, jnp.bfloat16
    hbm = [
        pltpu.with_memory_space_constraint(a, pltpu.HBM)
        for a in (wq, wk, wv, lq.T, lk.T, lv.T, hq, hk, hv, train.reshape(1, 32), step.reshape(1, 32))
    ]
    factors, norm, full = pl.pallas_call(
        gather_kernel,
        out_shape=(
            jax.ShapeDtypeStruct((24, 128), f32),
            jax.ShapeDtypeStruct((32, 128), bf16),
            pltpu.VMEM((3, D_MODEL, COLS), bf16),
        ),
        in_specs=[any_spec] * 9 + [vmem] * 2,
        out_specs=(vmem, vmem, vmem),
        scratch_shapes=[
            pltpu.VMEM((3, ROWS, COLS), bf16),
            pltpu.VMEM((3, 16, ROWS), bf16),
            pltpu.VMEM((3, 16, COLS), bf16),
            pltpu.VMEM((3, ROWS, COLS), f32),
            pltpu.VMEM((32, 128), f32),
            pltpu.VMEM((4, 8, 128), f32),
            pltpu.VMEM((32, 128), f32),
            pltpu.VMEM((4, 32, 128), f32),
            pltpu.VMEM((4, 32, 128), f32),
            pltpu.SemaphoreType.DMA((9,)),
            pltpu.SemaphoreType.DMA((10,)),
            pltpu.SemaphoreType.DMA((10,)),
            pltpu.SemaphoreType.DMA((N_SLOTS * 4,)),
            pltpu.SemaphoreType.DMA((N_SLOTS * 4,)),
            pltpu.SemaphoreType.DMA((N_SLOTS * 4,)),
            pltpu.SemaphoreType.DMA((N_SLOTS * 4,)),
            pltpu.SemaphoreType.DMA,
            pltpu.SemaphoreType.DMA,
        ],
        compiler_params=pltpu.CompilerParams(
            collective_id=0, has_side_effects=True, vmem_limit_bytes=16 * 1024 * 1024
        ),
    )(*hbm)
    query, key, value, f_query, f_key, f_value, norm = pl.pallas_call(
        write_kernel,
        out_shape=(
            jax.ShapeDtypeStruct((D_MODEL, COLS), bf16),
            jax.ShapeDtypeStruct((D_MODEL, COLS), bf16),
            jax.ShapeDtypeStruct((D_MODEL, COLS), bf16),
            jax.ShapeDtypeStruct((8, 128), f32),
            jax.ShapeDtypeStruct((8, 128), f32),
            jax.ShapeDtypeStruct((8, 128), f32),
            jax.ShapeDtypeStruct((32, 128), bf16),
        ),
        in_specs=[vmem] * 3,
        out_specs=[any_spec] * 3 + [vmem] * 4,
        scratch_shapes=[pltpu.SemaphoreType.DMA((12,))],
        compiler_params=pltpu.CompilerParams(vmem_limit_bytes=16 * 1024 * 1024),
    )(factors, norm, full)
    return (
        query, key, value,
        f_query.reshape(COLS), f_key.reshape(COLS), f_value.reshape(COLS), norm.reshape(D_MODEL),
    )


def solution(mesh):
    return jax.shard_map(
        per_device,
        mesh=mesh,
        in_specs=(
            P("zero", "model"), P("zero", None), P(None, "model"),
            P("zero", "model"), P("zero", None), P(None, "model"),
            P("zero", "model"), P("zero", None), P(None, "model"),
            P(("zero", "model")), P(("zero", "model")),
        ),
        out_specs=(
            P(None, "model"), P(None, "model"), P(None, "model"),
            P("model"), P("model"), P("model"), P(),
        ),
        check_vma=False,
    )
```

time: 147 us -> 99.2 us (0.67)
  Pallas kernels: 0 us -> 98.4 us
  waiting for transfers between devices: 56.7 us -> 0 us
  blocking collectives: 50.4 us -> 0 us
  local copies, waits for them, and re-layouts: 19.5 us -> 0 us
  between operations: 14.9 us -> 0.64 us
  matrix products: 3.76 us -> 0 us
    pallas_call x0 -> x2, Pallas kernels: none -> 98.4 us  [the longest x1 89.3 us: per_device(): pl.pallas_call(gather_kernel, out_shape=(jax.ShapeDtypeStruct((24, 128),...]
    all_gather x1 -> x0, waiting for transfers between devices: 56.7 us -> none  [sent_together(): out = lax.all_gather(both, axis, axis=dim, tiled=True)]
    all_gather x3 -> x0, blocking collectives: 24.2 us -> none  [gather_in_order(): tiles = lax.all_gather(tiles, axes[k])]
    all_to_all x1 -> x0, blocking collectives: 19.4 us -> none  [copy_for_each(): return lax.all_to_all(copies, axis, split_axis=0, concat_axis=0, tiled=True)]
    split x1 -> x0, local copies, waits for them, and re-layouts: 17 us -> none  [sent_together(): jnp.split(out, [sum(widths[:k]) for k in range(1, len(widths))], axis=along)]
    unnamed x1 -> x0, blocking collectives: 6.84 us -> none
    dot_general x3 -> x0, matrix products: 3.76 us -> none  [the longest x1 1.26 us: per_device(): jnp.dot(low_key, high_key, preferred_element_type=jnp.float32)]
    unnamed x18 -> x0, local copies, waits for them, and re-layouts: 1.63 us -> none
  transfers between devices with their start and end apart: 1 -> 0, of which waited for: 1 -> 0; matrix products, arithmetic and copies ran while one was open for 1% -> 0% of each run, Pallas kernels for 0% -> 0%
where the time goes in v1:
time: 99.2 us; the launch traced here: 99.1 us
  Pallas kernels  98.4 us (99%)
    pallas_call x1, Pallas kernels, per_device(): pl.pallas_call(gather_kernel, out_shape=(jax.ShapeDtypeStruct((24, 128),...  89.3 us
    pallas_call x1, Pallas kernels, per_device(): pl.pallas_call(write_kernel, out_shape=(jax.ShapeDtypeStruct((D_MODEL, CO...  9.09 us

profile of v1, /device:TPU:1, one launch (start us, length us, event | category | flops | bytes accessed | tf_op | source)
XLA Modules:
  0.0 99.1 jit_solution(7795968669524941600)
XLA Ops:
  0.6 89.3 %shard_map.162 = (f32[24,128]{1,0:T(8,128)S(1)}, bf16[32,128]{1,0:T(8,128)(2,1)S(1)}, bf16[3,4096,1024]{2,1,0:T(8,128)(2,1)S(1)}) custom-call(bf16[128,1024]{1,0:T(8,128)(2,1)} %w_query.1, bf16[128,1024]{1,0:T(8,128)(2,1)} %w_key.1, bf16[128,1024]{1,0:T(8,128)(2,1)} %w_value.1, bf16[16,128]{1,0:T(8,128)(2,1)} %bitcast.9, bf16[16,128]{1,0:T(8,128)(2,1)} %bitcast.10, ...), custom_call_target="tpu_custom_call" | custom-call | tf_op jit(solution)/shard_map/pallas_call | solution.py:240
  90.0 9.1 %shard_map.163 = (bf16[4096,1024]{1,0:T(8,128)(2,1)}, bf16[4096,1024]{1,0:T(8,128)(2,1)}, bf16[4096,1024]{1,0:T(8,128)(2,1)}, f32[8,128]{1,0:T(8,128)}, f32[8,12...) custom-call(f32[24,128]{1,0:T(8,128)S(1)} %get-tuple-element.17.factors, ...), custom_call_target="tpu_custom_call" | custom-call | tf_op jit(solution)/shard_map/pallas_call | solution.py:273

commit v2 on v1

v2 whole, which is shorter than its diff:
```python
import jax
import jax.numpy as jnp
from jax import lax
from jax.experimental import pallas as pl
from jax.experimental.pallas import tpu as pltpu
from jax.sharding import PartitionSpec as P

MESH = pl.DeviceIdType.MESH
D_MODEL = 4096
COLS = 1024
ROWS = 128
SUB = 32
SIDE = 4
GATHER_LIMIT = 16
WRITE_LIMIT = 18

MESSAGES = (
    (0, 0, 0, 2),
    (0, 0, 1, 2),
    (-1, 0, 0, 1),
    (0, -1, 1, 2),
    (0, 1, 1, 2),
    (0, 2, 1, 2),
    (-1, 0, 1, 1),
    (-1, -1, 1, 1),
    (-1, 1, 1, 1),
    (-1, 2, 1, 1),
)
N_MESSAGES = len(MESSAGES)


def scaled(low_rows, mixes, inverse, rows, start, source, store):
    low = low_rows[pl.ds(start, rows), :]
    for m in range(3):
        for pair in range(4):
            cols = slice(pair * 256, pair * 256 + 256)
            product = jnp.dot(low, mixes[m, :, cols], preferred_element_type=jnp.float32)
            for j in range(2):
                at = pair * 256 + j * 128
                row = m * 8 + pair * 2 + j
                whole = source[m, pl.ds(start, rows), at : at + 128].astype(jnp.float32) + product[:, j * 128 : j * 128 + 128]
                store(m, at, (whole * inverse[row : row + 1, :]).astype(jnp.bfloat16))


def gather_kernel(
    w_query, w_key, w_value, low_query, low_key, low_value, high_query, high_key, high_value, train, step,
    factors, inverse, norm, low_rows, mixes, full,
    lows, highs, message, from_y, from_core, from_first, from_second,
    load_sem, small_send, small_recv, send_sem, recv_sem, pass_send, pass_recv, own_send, own_recv,
):
    zero, y = lax.axis_index("zero"), lax.axis_index("model")
    z, x, core = zero // 8, zero // 2 % 4, zero % 2
    partner = zero + 1 - 2 * core
    own = pl.multiple_of(zero * ROWS, ROWS)
    first = x + core * (z - x)
    second = z + core * (x - z)

    def index_of(z_at, x_at, core_at):
        return (z_at * 4 + x_at) * 2 + core_at

    def peer(axis, k):
        return index_of((z + axis * k) % 4, (x + (1 - axis) * k) % 4, core)

    def remote(src, dst, sems, at, target, y_at):
        return pltpu.make_async_remote_copy(
            src_ref=src, dst_ref=dst, send_sem=sems[0].at[at], recv_sem=sems[1].at[at],
            device_id=(target, y_at), device_id_type=MESH,
        )

    small = (small_send, small_recv)
    place = second * 4 + first
    loads = [
        pltpu.make_async_copy(src, dst, load_sem.at[k])
        for k, (src, dst) in enumerate(
            (
                (w_query, full.at[0, pl.ds(own, ROWS), :]),
                (w_key, full.at[1, pl.ds(own, ROWS), :]),
                (w_value, full.at[2, pl.ds(own, ROWS), :]),
                (low_query, lows.at[core, place, pl.ds(0, 16), :]),
                (low_key, lows.at[core, place, pl.ds(16, 16), :]),
                (low_value, lows.at[core, place, pl.ds(32, 16), :]),
                (high_query, highs.at[0]), (high_key, highs.at[1]), (high_value, highs.at[2]),
            )
        )
    ]
    for load in loads:
        load.start()

    barrier = pltpu.get_barrier_semaphore()
    pl.semaphore_signal(barrier, inc=1, device_id=(partner, y), device_id_type=MESH)
    for k in range(1, SIDE):
        pl.semaphore_signal(barrier, inc=1, device_id=(peer(0, k), y), device_id_type=MESH)
        pl.semaphore_signal(barrier, inc=1, device_id=(peer(1, k), y), device_id_type=MESH)
        pl.semaphore_signal(barrier, inc=1, device_id=(zero, (y + k) % 4), device_id_type=MESH)

    gain = train[...] + step[...]
    gain = pltpu.roll(jnp.concatenate([gain, jnp.zeros((1, 96), jnp.float32)], axis=1), 32 * y, 1)
    row = lax.broadcasted_iota(jnp.int32, (8, 128), 0)
    tile = jnp.where(row == x * 2 + core, jnp.broadcast_to(gain, (8, 128)), 0.0)
    from_y[pl.ds(y, 1)] = tile[None]
    for load in loads[:3]:
        load.wait()
    pl.semaphore_wait(barrier, 10)

    def rows_of(link, at, arriving, core_at):
        along, across, half, parts = MESSAGES[at]
        axis, way = link // 2, 1 - 2 * (link % 2)
        along = (along - arriving) * way
        z_at = (z + axis * along + (1 - axis) * across + 8) % 4
        x_at = (x + (1 - axis) * along + axis * across + 8) % 4
        half = axis if half == 0 else 1 - axis
        part = link % 2 if parts == 1 else 0
        return pl.multiple_of(index_of(z_at, x_at, core_at) * ROWS + half * 64 + part * SUB, SUB)

    def chunk_of(link, at, arriving, core_at):
        return full.at[:, pl.ds(rows_of(link, at, arriving, core_at), MESSAGES[at][3] * SUB), :]

    def link_copy(link, at, arriving=0):
        axis, way = link // 2, 1 - 2 * (link % 2)
        chunk = chunk_of(link, at, arriving, core)
        target = index_of((z + axis * way + 4) % 4, (x + (1 - axis) * way + 4) % 4, core)
        return remote(chunk, chunk, (send_sem, recv_sem), at * 4 + link, target, y)

    def pass_copy(link, at, arriving_from=None):
        chunk = chunk_of(link, at, 1, core)
        return remote(chunk, chunk, (pass_send, pass_recv), at * 4 + link, partner, y)

    def each_link(body, count=4):
        def step_of(link, carry):
            body(link)
            return carry

        lax.fori_loop(0, count, step_of, 0)

    def send(at):
        each_link(lambda link: link_copy(link, at).start())

    def arrive(at):
        def body(link):
            link_copy(link, at, 1).wait_recv()
            pass_copy(link, at).start()

        each_link(body)

    send(0)
    block = full.at[:, pl.ds(own, ROWS), :]
    own_copy = pltpu.make_async_remote_copy(
        src_ref=block, dst_ref=block, send_sem=own_send, recv_sem=own_recv,
        device_id=(partner, y), device_id_type=MESH,
    )
    own_copy.start()
    y_copies = [
        remote(from_y.at[y], from_y.at[y], small, k, zero, (y + k) % 4) for k in range(1, SIDE)
    ]
    for copy in y_copies:
        copy.start()

    for load in loads[3:]:
        load.wait()
    low_own = lows.at[core, place]
    low_first = [remote(low_own, low_own, small, 10 + k, peer(core, k), y) for k in range(1, SIDE)]
    for copy in low_first:
        copy.start()
    send(1)
    for m in range(3):
        product = lax.dot_general(
            low_own[16 * m : 16 * m + 16, :], highs[m], (((0,), (0,)), ((), ())),
            preferred_element_type=jnp.float32,
        )
        value = full[m, pl.ds(own, ROWS), :].astype(jnp.float32) + 0.5 * product
        total = jnp.sum(jnp.abs(value), axis=0, keepdims=True)
        for j in range(8):
            message[m * 8 + j : m * 8 + j + 1, :] = total[:, j * 128 : (j + 1) * 128]
        mixes[m] = jnp.zeros((128, COLS), jnp.bfloat16)
        mixes[m, 16 * m : 16 * m + 16, :] = (0.5 * highs[m].astype(jnp.float32)).astype(jnp.bfloat16)
    for copy in y_copies:
        copy.wait()
    message[24:32, :] = from_y[0] + from_y[1] + from_y[2] + from_y[3]

    core_copy = remote(message, from_core, small, 0, partner, y)
    core_copy.start()
    core_copy.wait()
    share = 1 - core
    mine = pl.ds(pl.multiple_of(share * 16, 16), 16)
    from_first[pl.ds(first, 1)] = (message[mine, :] + from_core[mine, :])[None]
    first_copies = [
        remote(from_first.at[first], from_first.at[first], small, 3 + k, peer(core, k), y)
        for k in range(1, SIDE)
    ]
    for copy in first_copies:
        copy.start()

    arrive(0)
    send(2)
    send(3)
    for copy in first_copies + low_first:
        copy.wait()
    from_second[pl.ds(share, 1), pl.ds(second, 1)] = (
        from_first[0] + from_first[1] + from_first[2] + from_first[3]
    )[None, None]
    own_sum = from_second.at[share, second]
    second_copies = [remote(own_sum, own_sum, small, 6 + k, peer(1 - core, k), y) for k in range(1, SIDE)]
    low_line = lows.at[core, pl.ds(pl.multiple_of(second * 4, 4), 4)]
    second_copies += [remote(low_line, low_line, small, 13 + k, peer(1 - core, k), y) for k in range(1, SIDE)]
    for copy in second_copies:
        copy.start()

    arrive(1)
    send(4)
    for copy in second_copies:
        copy.wait()
    last_copies = [
        remote(from_second.at[share], from_second.at[share], small, 10, partner, y),
        remote(lows.at[core], lows.at[core], small, 17, partner, y),
    ]
    for copy in last_copies:
        copy.start()
    for copy in last_copies:
        copy.wait()
    sums = [from_second[h, 0] + from_second[h, 1] + from_second[h, 2] + from_second[h, 3] for h in range(2)]
    factor = jnp.concatenate([sums[0], sums[1][:8]], axis=0) / D_MODEL
    factors[...] = factor
    inverse[...] = 1.0 / factor
    for k in range(SIDE):
        norm[k * 8 : (k + 1) * 8, :] = from_second[1, k, 8:16, :].astype(jnp.bfloat16)

    arrive(2)
    send(5)
    lane = lax.broadcasted_iota(jnp.int32, (48, 128), 1)
    unit = jnp.where(lax.broadcasted_iota(jnp.int32, (48, 128), 0) == lane, 1.0, 0.0).astype(jnp.bfloat16)

    def turn(k, carry):
        core_at, major, minor = k // 16, k // 4 % 4, k % 4
        z_at = major + core_at * (minor - major)
        x_at = minor + core_at * (major - minor)
        start = pl.multiple_of(index_of(z_at, x_at, core_at) * ROWS, ROWS)
        turned = lax.dot_general(
            lows[core_at, k % 16], unit, (((0,), (0,)), ((), ())), preferred_element_type=jnp.float32
        )
        low_rows[pl.ds(start, ROWS), :] = turned.astype(jnp.bfloat16)
        return carry

    lax.fori_loop(0, 32, turn, 0)

    scale = inverse[...]

    def scale_rows(start):
        def store(m, at, value):
            full[m, pl.ds(start, 64), at : at + 128] = value

        scaled(low_rows, mixes, scale, 64, start, full, store)

    def scale_passed(at):
        def body(link):
            pass_copy(link, at).wait_recv()
            scale_rows(pl.multiple_of(rows_of(link, at, 1, 1 - core), 64))

        each_link(body)

    own_copy.wait_recv()
    each_link(lambda half: scale_rows(pl.multiple_of(partner * ROWS + half * 64, 64)), 2)
    scale_passed(0)
    arrive(3)
    send(6)
    send(7)
    scale_passed(1)

    def both_parts(axis):
        pass_copy(2 * axis, 2).wait_recv()
        pass_copy(2 * axis + 1, 2).wait_recv()
        scale_rows(pl.multiple_of(rows_of(2 * axis, 2, 1, 1 - core), 64))

    each_link(both_parts, 2)
    arrive(4)
    send(8)
    scale_passed(3)
    arrive(5)
    send(9)
    scale_passed(4)
    arrive(6)
    scale_passed(5)
    arrive(7)
    arrive(8)
    arrive(9)
    for at in range(N_MESSAGES):

        def finish(link):
            link_copy(link, at).wait_send()
            pass_copy(link, at).wait_send()
            if at > 5:
                pass_copy(link, at).wait_recv()

        each_link(finish)
    own_copy.wait_send()


def write_kernel(
    factors, inverse, norm, low_rows, mixes, full,
    query, key, value, f_query, f_key, f_value, norm_out, mine, late, sem,
):
    zero = lax.axis_index("zero")
    z, x, core = zero // 8, zero // 2 % 4, zero % 2
    outs = (query, key, value)

    def index_of(z_at, x_at, core_at):
        return (z_at * 4 + x_at) * 2 + core_at

    def ready_start(k):
        half, far, near = k // 12, k // 4 % 3, k % 4
        far = far + 3
        z_at = (z + (1 - half) * far + half * near) % 4
        x_at = (x + half * far + (1 - half) * near) % 4
        return pl.multiple_of(index_of(z_at, x_at, 1 - core) * ROWS + half * 64, 64)

    def late_start(k):
        half, near = k // 4, k % 4
        z_at = (z + (1 - half) * 2 + half * near) % 4
        x_at = (x + half * 2 + (1 - half) * near) % 4
        return pl.multiple_of(index_of(z_at, x_at, 1 - core) * ROWS + half * 64, 64)

    def mine_start(k):
        return pl.multiple_of((k * 2 + core) * ROWS, ROWS)

    def ready_copy(k, m):
        rows = pl.ds(ready_start(k), 64)
        return pltpu.make_async_copy(full.at[m, rows, :], outs[m].at[rows, :], sem.at[k * 3 + m])

    def mine_copy(k, m):
        return pltpu.make_async_copy(mine.at[k, m], outs[m].at[pl.ds(mine_start(k), ROWS), :], sem.at[72 + k * 3 + m])

    def late_copy(k, m):
        return pltpu.make_async_copy(late.at[k, m], outs[m].at[pl.ds(late_start(k), 64), :], sem.at[120 + k * 3 + m])

    def each(count, body):
        def step_of(k, carry):
            body(k)
            return carry

        lax.fori_loop(0, count, step_of, 0)

    def start_all(copy):
        def body(k):
            for m in range(3):
                copy(k, m).start()

        return body

    def wait_all(copy):
        def body(k):
            for m in range(3):
                copy(k, m).wait()

        return body

    each(24, start_all(ready_copy))
    for m, out in enumerate((f_query, f_key, f_value)):
        out[...] = factors[m * 8 : (m + 1) * 8, :]
    norm_out[...] = norm[...]
    scale = inverse[...]

    def scale_mine(k):
        def store(m, at, value):
            mine[k, m, :, at : at + 128] = value

        scaled(low_rows, mixes, scale, ROWS, mine_start(k), full, store)
        start_all(mine_copy)(k)

    def scale_late(k):
        def store(m, at, value):
            late[k, m, :, at : at + 128] = value

        scaled(low_rows, mixes, scale, 64, late_start(k), full, store)
        start_all(late_copy)(k)

    each(16, scale_mine)
    each(8, scale_late)
    each(24, wait_all(ready_copy))
    each(16, wait_all(mine_copy))
    each(8, wait_all(late_copy))


def per_device(wq, lq, hq, wk, lk, hk, wv, lv, hv, train, step):
    any_spec = pl.BlockSpec(memory_space=pl.ANY)
    vmem = pl.BlockSpec(memory_space=pltpu.VMEM)
    f32, bf16 = jnp.float32, jnp.bfloat16
    hbm = [
        pltpu.with_memory_space_constraint(a, pltpu.HBM)
        for a in (wq, wk, wv, lq.T, lk.T, lv.T, hq, hk, hv, train.reshape(1, 32), step.reshape(1, 32))
    ]
    state = pl.pallas_call(
        gather_kernel,
        out_shape=(
            jax.ShapeDtypeStruct((24, 128), f32),
            jax.ShapeDtypeStruct((24, 128), f32),
            jax.ShapeDtypeStruct((32, 128), bf16),
            pltpu.VMEM((D_MODEL, 128), bf16),
            pltpu.VMEM((3, 128, COLS), bf16),
            pltpu.VMEM((3, D_MODEL, COLS), bf16),
        ),
        in_specs=[any_spec] * 9 + [vmem] * 2,
        out_specs=(vmem,) * 6,
        scratch_shapes=[
            pltpu.VMEM((2, 16, 48, 128), bf16),
            pltpu.VMEM((3, 16, COLS), bf16),
            pltpu.VMEM((32, 128), f32),
            pltpu.VMEM((4, 8, 128), f32),
            pltpu.VMEM((32, 128), f32),
            pltpu.VMEM((4, 16, 128), f32),
            pltpu.VMEM((2, 4, 16, 128), f32),
            pltpu.SemaphoreType.DMA((9,)),
            pltpu.SemaphoreType.DMA((18,)),
            pltpu.SemaphoreType.DMA((18,)),
            pltpu.SemaphoreType.DMA((N_MESSAGES * 4,)),
            pltpu.SemaphoreType.DMA((N_MESSAGES * 4,)),
            pltpu.SemaphoreType.DMA((N_MESSAGES * 4,)),
            pltpu.SemaphoreType.DMA((N_MESSAGES * 4,)),
            pltpu.SemaphoreType.DMA,
            pltpu.SemaphoreType.DMA,
        ],
        compiler_params=pltpu.CompilerParams(
            collective_id=0, has_side_effects=True, vmem_limit_bytes=GATHER_LIMIT * 1024 * 1024
        ),
    )(*hbm)
    query, key, value, f_query, f_key, f_value, norm = pl.pallas_call(
        write_kernel,
        out_shape=(
            jax.ShapeDtypeStruct((D_MODEL, COLS), bf16),
            jax.ShapeDtypeStruct((D_MODEL, COLS), bf16),
            jax.ShapeDtypeStruct((D_MODEL, COLS), bf16),
            jax.ShapeDtypeStruct((8, 128), f32),
            jax.ShapeDtypeStruct((8, 128), f32),
            jax.ShapeDtypeStruct((8, 128), f32),
            jax.ShapeDtypeStruct((32, 128), bf16),
        ),
        in_specs=[vmem] * 6,
        out_specs=[any_spec] * 3 + [vmem] * 4,
        scratch_shapes=[
            pltpu.VMEM((16, 3, ROWS, COLS), bf16),
            pltpu.VMEM((8, 3, 64, COLS), bf16),
            pltpu.SemaphoreType.DMA((144,)),
        ],
        compiler_params=pltpu.CompilerParams(vmem_limit_bytes=WRITE_LIMIT * 1024 * 1024),
    )(*state)
    return (
        query, key, value,
        f_query.reshape(COLS), f_key.reshape(COLS), f_value.reshape(COLS), norm.reshape(D_MODEL),
    )


def solution(mesh):
    return jax.shard_map(
        per_device,
        mesh=mesh,
        in_specs=(
            P("zero", "model"), P("zero", None), P(None, "model"),
            P("zero", "model"), P("zero", None), P(None, "model"),
            P("zero", "model"), P("zero", None), P(None, "model"),
            P(("zero", "model")), P(("zero", "model")),
        ),
        out_specs=(
            P(None, "model"), P(None, "model"), P(None, "model"),
            P("model"), P("model"), P("model"), P(),
        ),
        check_vma=False,
    )
```

time: 99.2 us -> 90.3 us (0.910)
  Pallas kernels: 98.4 us -> 89.5 us
    pallas_call x1, Pallas kernels: 89.3 us -> 77.9 us  [per_device(): pl.pallas_call(gather_kernel, out_shape=(jax.ShapeDtypeStruct((24, 128),...]
    pallas_call x1, Pallas kernels: 9.09 us -> 11.6 us  [per_device(): pl.pallas_call(write_kernel, out_shape=(jax.ShapeDtypeStruct((D_MODEL, CO...]
where the time goes in v2:
time: 90.3 us; the launch traced here: 90.2 us
  Pallas kernels  89.5 us (99%)
    pallas_call x1, Pallas kernels, per_device(): pl.pallas_call(gather_kernel, out_shape=(jax.ShapeDtypeStruct((24, 128),...  77.9 us
    pallas_call x1, Pallas kernels, per_device(): pl.pallas_call(write_kernel, out_shape=(jax.ShapeDtypeStruct((D_MODEL, CO...  11.6 us

profile of v2, /device:TPU:1, one launch (start us, length us, event | category | flops | bytes accessed | tf_op | source)
XLA Modules:
  0.0 90.2 jit_solution(17747074381753638310)
XLA Ops:
  0.6 77.9 %shard_map.162 = (f32[24,128]{1,0:T(8,128)S(1)}, f32[24,128]{1,0:T(8,128)S(1)}, bf16[32,128]{1,0:T(8,128)(2,1)S(1)}, bf16[4096,128]{1,0:T(8,128)(2,1)S(1)}, bf16...) custom-call(bf16[128,1024]{1,0:T(8,128)(2,1)} %w_query.1, bf16[128,1024]{1,0:T(8,128)(2,1)} %w_key.1, ...), custom_call_target="tpu_custom_call" | custom-call | tf_op jit(solution)/shard_map/pallas_call | solution.py:390
  78.6 11.6 %shard_map.163 = (bf16[4096,1024]{1,0:T(8,128)(2,1)}, bf16[4096,1024]{1,0:T(8,128)(2,1)}, bf16[4096,1024]{1,0:T(8,128)(2,1)}, f32[8,128]{1,0:T(8,128)}, f32[8,12...) custom-call(f32[24,128]{1,0:T(8,128)S(1)} %get-tuple-element.20.factors, ...), custom_call_target="tpu_custom_call" | custom-call | tf_op jit(solution)/shard_map/pallas_call | solution.py:424

commit v3 on v2

--- a/solution.py
+++ b/solution.py
@@ -12,7 +12,7 @@
 SUB = 32
 SIDE = 4
 GATHER_LIMIT = 16
-WRITE_LIMIT = 18
+WRITE_LIMIT = 16
 
 MESSAGES = (
     (0, 0, 0, 2),
@@ -121,7 +121,7 @@
         target = index_of((z + axis * way + 4) % 4, (x + (1 - axis) * way + 4) % 4, core)
         return remote(chunk, chunk, (send_sem, recv_sem), at * 4 + link, target, y)
 
-    def pass_copy(link, at, arriving_from=None):
+    def pass_copy(link, at):
         chunk = chunk_of(link, at, 1, core)
         return remote(chunk, chunk, (pass_send, pass_recv), at * 4 + link, partner, y)
 
@@ -257,126 +257,125 @@
 
         each_link(body)
 
+    def scale_passed_pair(at):
+        def body(axis):
+            pass_copy(2 * axis, at).wait_recv()
+            pass_copy(2 * axis + 1, at).wait_recv()
+            scale_rows(pl.multiple_of(rows_of(2 * axis, at, 1, 1 - core), 64))
+
+        each_link(body, 2)
+
+    def scale_mine(at):
+        def body(link):
+            pass_copy(link, at).wait_send()
+            scale_rows(pl.multiple_of(rows_of(link, at, 1, core), 64))
+
+        each_link(body)
+
+    def scale_mine_pair(at):
+        def body(axis):
+            pass_copy(2 * axis, at).wait_send()
+            pass_copy(2 * axis + 1, at).wait_send()
+            scale_rows(pl.multiple_of(rows_of(2 * axis, at, 1, core), 64))
+
+        each_link(body, 2)
+
+    def sent(at):
+        each_link(lambda link: link_copy(link, at).wait_send())
+
     own_copy.wait_recv()
     each_link(lambda half: scale_rows(pl.multiple_of(partner * ROWS + half * 64, 64)), 2)
     scale_passed(0)
+    sent(0)
+    sent(1)
+    own_copy.wait_send()
+    each_link(lambda half: scale_rows(pl.multiple_of(zero * ROWS + half * 64, 64)), 2)
     arrive(3)
     send(6)
     send(7)
     scale_passed(1)
-
-    def both_parts(axis):
-        pass_copy(2 * axis, 2).wait_recv()
-        pass_copy(2 * axis + 1, 2).wait_recv()
-        scale_rows(pl.multiple_of(rows_of(2 * axis, 2, 1, 1 - core), 64))
-
-    each_link(both_parts, 2)
+    scale_passed_pair(2)
     arrive(4)
     send(8)
     scale_passed(3)
+    sent(2)
+    sent(3)
+    sent(4)
+    scale_mine(0)
     arrive(5)
     send(9)
     scale_passed(4)
+    sent(5)
+    scale_mine_pair(2)
     arrive(6)
+    sent(6)
+    scale_mine(1)
     scale_passed(5)
     arrive(7)
+    sent(7)
+    scale_mine(3)
+    scale_mine_pair(6)
+    scale_passed_pair(6)
     arrive(8)
+    sent(8)
+    scale_mine(4)
+    scale_mine_pair(7)
+    scale_passed_pair(7)
     arrive(9)
-    for at in range(N_MESSAGES):
-
-        def finish(link):
-            link_copy(link, at).wait_send()
-            pass_copy(link, at).wait_send()
-            if at > 5:
-                pass_copy(link, at).wait_recv()
-
-        each_link(finish)
-    own_copy.wait_send()
+    sent(9)
+    scale_mine(5)
+    scale_mine_pair(8)
+    scale_passed_pair(8)
+    each_link(lambda link: pass_copy(link, 9).wait())
 
 
 def write_kernel(
     factors, inverse, norm, low_rows, mixes, full,
-    query, key, value, f_query, f_key, f_value, norm_out, mine, late, sem,
+    query, key, value, f_query, f_key, f_value, norm_out, late, sem,
 ):
     zero = lax.axis_index("zero")
-    z, x, core = zero // 8, zero // 2 % 4, zero % 2
+    z, x = zero // 8, zero // 2 % 4
     outs = (query, key, value)
 
-    def index_of(z_at, x_at, core_at):
-        return (z_at * 4 + x_at) * 2 + core_at
-
-    def ready_start(k):
-        half, far, near = k // 12, k // 4 % 3, k % 4
-        far = far + 3
-        z_at = (z + (1 - half) * far + half * near) % 4
-        x_at = (x + half * far + (1 - half) * near) % 4
-        return pl.multiple_of(index_of(z_at, x_at, 1 - core) * ROWS + half * 64, 64)
-
-    def late_start(k):
-        half, near = k // 4, k % 4
-        z_at = (z + (1 - half) * 2 + half * near) % 4
-        x_at = (x + half * 2 + (1 - half) * near) % 4
-        return pl.multiple_of(index_of(z_at, x_at, 1 - core) * ROWS + half * 64, 64)
-
-    def mine_start(k):
-        return pl.multiple_of((k * 2 + core) * ROWS, ROWS)
+    def start_of(k):
+        return pl.multiple_of(((z + 2 + k // 4) % 4 * 4 + (x + 2 + k % 4) % 4) * 2 * ROWS, 2 * ROWS)
 
     def ready_copy(k, m):
-        rows = pl.ds(ready_start(k), 64)
+        rows = pl.ds(start_of(k), 2 * ROWS)
         return pltpu.make_async_copy(full.at[m, rows, :], outs[m].at[rows, :], sem.at[k * 3 + m])
 
-    def mine_copy(k, m):
-        return pltpu.make_async_copy(mine.at[k, m], outs[m].at[pl.ds(mine_start(k), ROWS), :], sem.at[72 + k * 3 + m])
-
-    def late_copy(k, m):
-        return pltpu.make_async_copy(late.at[k, m], outs[m].at[pl.ds(late_start(k), 64), :], sem.at[120 + k * 3 + m])
-
-    def each(count, body):
-        def step_of(k, carry):
-            body(k)
-            return carry
-
-        lax.fori_loop(0, count, step_of, 0)
-
-    def start_all(copy):
-        def body(k):
-            for m in range(3):
-                copy(k, m).start()
-
-        return body
-
-    def wait_all(copy):
-        def body(k):
-            for m in range(3):
-                copy(k, m).wait()
-
-        return body
-
-    each(24, start_all(ready_copy))
+    def late_copy(m):
+        return pltpu.make_async_copy(late.at[m], outs[m].at[pl.ds(start_of(0), 2 * ROWS), :], sem.at[m])
+
+    def start_ready(k, carry):
+        for m in range(3):
+            ready_copy(k, m).start()
+        return carry
+
+    def wait_ready(k, carry):
+        for m in range(3):
+            ready_copy(k, m).wait()
+        return carry
+
+    lax.fori_loop(1, 16, start_ready, 0)
     for m, out in enumerate((f_query, f_key, f_value)):
         out[...] = factors[m * 8 : (m + 1) * 8, :]
     norm_out[...] = norm[...]
     scale = inverse[...]
 
-    def scale_mine(k):
+    def scale_late(k, carry):
         def store(m, at, value):
-            mine[k, m, :, at : at + 128] = value
-
-        scaled(low_rows, mixes, scale, ROWS, mine_start(k), full, store)
-        start_all(mine_copy)(k)
-
-    def scale_late(k):
-        def store(m, at, value):
-            late[k, m, :, at : at + 128] = value
-
-        scaled(low_rows, mixes, scale, 64, late_start(k), full, store)
-        start_all(late_copy)(k)
-
-    each(16, scale_mine)
-    each(8, scale_late)
-    each(24, wait_all(ready_copy))
-    each(16, wait_all(mine_copy))
-    each(8, wait_all(late_copy))
+            late[m, pl.ds(pl.multiple_of(k * 64, 64), 64), at : at + 128] = value
+
+        scaled(low_rows, mixes, scale, 64, pl.multiple_of(start_of(0) + k * 64, 64), full, store)
+        return carry
+
+    lax.fori_loop(0, 4, scale_late, 0)
+    for m in range(3):
+        late_copy(m).start()
+    lax.fori_loop(1, 16, wait_ready, 0)
+    for m in range(3):
+        late_copy(m).wait()
 
 
 def per_device(wq, lq, hq, wk, lk, hk, wv, lv, hv, train, step):
@@ -435,9 +434,8 @@
         in_specs=[vmem] * 6,
         out_specs=[any_spec] * 3 + [vmem] * 4,
         scratch_shapes=[
-            pltpu.VMEM((16, 3, ROWS, COLS), bf16),
-            pltpu.VMEM((8, 3, 64, COLS), bf16),
-            pltpu.SemaphoreType.DMA((144,)),
+            pltpu.VMEM((3, 2 * ROWS, COLS), bf16),
+            pltpu.SemaphoreType.DMA((48,)),
         ],
         compiler_params=pltpu.CompilerParams(vmem_limit_bytes=WRITE_LIMIT * 1024 * 1024),
     )(*state)

time: 90.3 us -> 88.2 us (0.977)
  Pallas kernels: 89.5 us -> 87.4 us
    pallas_call x1, Pallas kernels: 11.6 us -> 9.39 us  [per_device(): pl.pallas_call(write_kernel, out_shape=(jax.ShapeDtypeStruct((D_MODEL, CO...]
where the time goes in v3:
time: 88.2 us; the launch traced here: 88 us
  Pallas kernels  87.4 us (99%)
    pallas_call x1, Pallas kernels, per_device(): pl.pallas_call(gather_kernel, out_shape=(jax.ShapeDtypeStruct((24, 128),...  78 us
    pallas_call x1, Pallas kernels, per_device(): pl.pallas_call(write_kernel, out_shape=(jax.ShapeDtypeStruct((D_MODEL, CO...  9.39 us

profile of v3, /device:TPU:1, one launch (start us, length us, event | category | flops | bytes accessed | tf_op | source)
XLA Modules:
  0.0 88.0 jit_solution(17277477148415762337)
XLA Ops:
  0.6 78.0 %shard_map.162 = (f32[24,128]{1,0:T(8,128)S(1)}, f32[24,128]{1,0:T(8,128)S(1)}, bf16[32,128]{1,0:T(8,128)(2,1)S(1)}, bf16[4096,128]{1,0:T(8,128)(2,1)S(1)}, bf16...) custom-call(bf16[128,1024]{1,0:T(8,128)(2,1)} %w_query.1, bf16[128,1024]{1,0:T(8,128)(2,1)} %w_key.1, ...), custom_call_target="tpu_custom_call" | custom-call | tf_op jit(solution)/shard_map/pallas_call | solution.py:389
  78.6 9.4 %shard_map.163 = (bf16[4096,1024]{1,0:T(8,128)(2,1)}, bf16[4096,1024]{1,0:T(8,128)(2,1)}, bf16[4096,1024]{1,0:T(8,128)(2,1)}, f32[8,128]{1,0:T(8,128)}, f32[8,12...) custom-call(f32[24,128]{1,0:T(8,128)S(1)} %get-tuple-element.20.factors, ...), custom_call_target="tpu_custom_call" | custom-call | tf_op jit(solution)/shard_map/pallas_call | solution.py:423

commit v4 on v3

--- a/solution.py
+++ b/solution.py
@@ -15,16 +15,16 @@
 WRITE_LIMIT = 16
 
 MESSAGES = (
-    (0, 0, 0, 2),
-    (0, 0, 1, 2),
-    (-1, 0, 0, 1),
-    (0, -1, 1, 2),
-    (0, 1, 1, 2),
-    (0, 2, 1, 2),
-    (-1, 0, 1, 1),
-    (-1, -1, 1, 1),
-    (-1, 1, 1, 1),
-    (-1, 2, 1, 1),
+    (0, 0, 0, 2, 0, 64),
+    (0, 0, 1, 2, 0, 64),
+    (-1, 0, 0, 1, 0, 32),
+    (0, -1, 1, 2, 0, 64),
+    (0, 1, 1, 2, 0, 64),
+    (0, 2, 1, 2, 0, 64),
+    (-1, 0, 1, 1, 0, 32),
+    (-1, -1, 1, 1, 0, 32),
+    (-1, 1, 1, 1, 0, 32),
+    (-1, 2, 1, 1, 0, 32),
 )
 N_MESSAGES = len(MESSAGES)
 
@@ -45,7 +45,7 @@
 def gather_kernel(
     w_query, w_key, w_value, low_query, low_key, low_value, high_query, high_key, high_value, train, step,
     factors, inverse, norm, low_rows, mixes, full,
-    lows, highs, message, from_y, from_core, from_first, from_second,
+    gains, low_own, lows, highs, message, from_y, from_core, from_first, from_second,
     load_sem, small_send, small_recv, send_sem, recv_sem, pass_send, pass_recv, own_send, own_recv,
 ):
     zero, y = lax.axis_index("zero"), lax.axis_index("model")
@@ -73,12 +73,11 @@
         pltpu.make_async_copy(src, dst, load_sem.at[k])
         for k, (src, dst) in enumerate(
             (
+                (train, gains.at[0]), (step, gains.at[1]),
                 (w_query, full.at[0, pl.ds(own, ROWS), :]),
                 (w_key, full.at[1, pl.ds(own, ROWS), :]),
                 (w_value, full.at[2, pl.ds(own, ROWS), :]),
-                (low_query, lows.at[core, place, pl.ds(0, 16), :]),
-                (low_key, lows.at[core, place, pl.ds(16, 16), :]),
-                (low_value, lows.at[core, place, pl.ds(32, 16), :]),
+                (low_query, low_own.at[0]), (low_key, low_own.at[1]), (low_value, low_own.at[2]),
                 (high_query, highs.at[0]), (high_key, highs.at[1]), (high_value, highs.at[2]),
             )
         )
@@ -93,27 +92,29 @@
         pl.semaphore_signal(barrier, inc=1, device_id=(peer(1, k), y), device_id_type=MESH)
         pl.semaphore_signal(barrier, inc=1, device_id=(zero, (y + k) % 4), device_id_type=MESH)
 
-    gain = train[...] + step[...]
+    for load in loads[:2]:
+        load.wait()
+    gain = gains[0] + gains[1]
     gain = pltpu.roll(jnp.concatenate([gain, jnp.zeros((1, 96), jnp.float32)], axis=1), 32 * y, 1)
     row = lax.broadcasted_iota(jnp.int32, (8, 128), 0)
     tile = jnp.where(row == x * 2 + core, jnp.broadcast_to(gain, (8, 128)), 0.0)
     from_y[pl.ds(y, 1)] = tile[None]
-    for load in loads[:3]:
+    for load in loads[2:5]:
         load.wait()
     pl.semaphore_wait(barrier, 10)
 
     def rows_of(link, at, arriving, core_at):
-        along, across, half, parts = MESSAGES[at]
+        along, across, half, parts, skip, _ = MESSAGES[at]
         axis, way = link // 2, 1 - 2 * (link % 2)
         along = (along - arriving) * way
         z_at = (z + axis * along + (1 - axis) * across + 8) % 4
         x_at = (x + (1 - axis) * along + axis * across + 8) % 4
         half = axis if half == 0 else 1 - axis
         part = link % 2 if parts == 1 else 0
-        return pl.multiple_of(index_of(z_at, x_at, core_at) * ROWS + half * 64 + part * SUB, SUB)
+        return pl.multiple_of(index_of(z_at, x_at, core_at) * ROWS + half * 64 + part * SUB + skip, 8)
 
     def chunk_of(link, at, arriving, core_at):
-        return full.at[:, pl.ds(rows_of(link, at, arriving, core_at), MESSAGES[at][3] * SUB), :]
+        return full.at[:, pl.ds(rows_of(link, at, arriving, core_at), MESSAGES[at][5]), :]
 
     def link_copy(link, at, arriving=0):
         axis, way = link // 2, 1 - 2 * (link % 2)
@@ -143,42 +144,33 @@
         each_link(body)
 
     send(0)
-    block = full.at[:, pl.ds(own, ROWS), :]
-    own_copy = pltpu.make_async_remote_copy(
-        src_ref=block, dst_ref=block, send_sem=own_send, recv_sem=own_recv,
-        device_id=(partner, y), device_id_type=MESH,
-    )
-    own_copy.start()
     y_copies = [
         remote(from_y.at[y], from_y.at[y], small, k, zero, (y + k) % 4) for k in range(1, SIDE)
     ]
     for copy in y_copies:
         copy.start()
 
-    for load in loads[3:]:
+    for load in loads[5:]:
         load.wait()
-    low_own = lows.at[core, place]
-    low_first = [remote(low_own, low_own, small, 10 + k, peer(core, k), y) for k in range(1, SIDE)]
-    for copy in low_first:
-        copy.start()
-    send(1)
+    lows[core, y, place] = low_own[y - y // 3]
     for m in range(3):
         product = lax.dot_general(
-            low_own[16 * m : 16 * m + 16, :], highs[m], (((0,), (0,)), ((), ())),
-            preferred_element_type=jnp.float32,
+            low_own[m], highs[m], (((0,), (0,)), ((), ())), preferred_element_type=jnp.float32
         )
         value = full[m, pl.ds(own, ROWS), :].astype(jnp.float32) + 0.5 * product
         total = jnp.sum(jnp.abs(value), axis=0, keepdims=True)
         for j in range(8):
             message[m * 8 + j : m * 8 + j + 1, :] = total[:, j * 128 : (j + 1) * 128]
-        mixes[m] = jnp.zeros((128, COLS), jnp.bfloat16)
-        mixes[m, 16 * m : 16 * m + 16, :] = (0.5 * highs[m].astype(jnp.float32)).astype(jnp.bfloat16)
     for copy in y_copies:
         copy.wait()
     message[24:32, :] = from_y[0] + from_y[1] + from_y[2] + from_y[3]
 
     core_copy = remote(message, from_core, small, 0, partner, y)
     core_copy.start()
+    low_block = lows.at[core, y, place]
+    low_first = [remote(low_block, low_block, small, 10 + k, peer(core, k), y) for k in range(1, SIDE)]
+    for copy in low_first:
+        copy.start()
     core_copy.wait()
     share = 1 - core
     mine = pl.ds(pl.multiple_of(share * 16, 16), 16)
@@ -189,10 +181,18 @@
     ]
     for copy in first_copies:
         copy.start()
+    send(1)
+    block = full.at[:, pl.ds(own, ROWS), :]
+    own_copy = pltpu.make_async_remote_copy(
+        src_ref=block, dst_ref=block, send_sem=own_send, recv_sem=own_recv,
+        device_id=(partner, y), device_id_type=MESH,
+    )
+    own_copy.start()
+    for m in range(3):
+        mixes[m] = jnp.zeros((128, COLS), jnp.bfloat16)
+        mixes[m, 16 * m : 16 * m + 16, :] = (0.5 * highs[m].astype(jnp.float32)).astype(jnp.bfloat16)
 
     arrive(0)
-    send(2)
-    send(3)
     for copy in first_copies + low_first:
         copy.wait()
     from_second[pl.ds(share, 1), pl.ds(second, 1)] = (
@@ -200,23 +200,24 @@
     )[None, None]
     own_sum = from_second.at[share, second]
     second_copies = [remote(own_sum, own_sum, small, 6 + k, peer(1 - core, k), y) for k in range(1, SIDE)]
-    low_line = lows.at[core, pl.ds(pl.multiple_of(second * 4, 4), 4)]
+    low_line = lows.at[core, y, pl.ds(pl.multiple_of(second * 4, 4), 4)]
     second_copies += [remote(low_line, low_line, small, 13 + k, peer(1 - core, k), y) for k in range(1, SIDE)]
     for copy in second_copies:
         copy.start()
+    send(2)
+    send(3)
 
     arrive(1)
     send(4)
     for copy in second_copies:
         copy.wait()
-    last_copies = [
-        remote(from_second.at[share], from_second.at[share], small, 10, partner, y),
-        remote(lows.at[core], lows.at[core], small, 17, partner, y),
-    ]
-    for copy in last_copies:
+    sum_copy = remote(from_second.at[share], from_second.at[share], small, 10, partner, y)
+    sum_copy.start()
+    low_plane = lows.at[core, y]
+    low_planes = [remote(low_plane, low_plane, small, 17 + k, zero, (y + k) % 4) for k in range(1, SIDE)]
+    for copy in low_planes:
         copy.start()
-    for copy in last_copies:
-        copy.wait()
+    sum_copy.wait()
     sums = [from_second[h, 0] + from_second[h, 1] + from_second[h, 2] + from_second[h, 3] for h in range(2)]
     factor = jnp.concatenate([sums[0], sums[1][:8]], axis=0) / D_MODEL
     factors[...] = factor
@@ -224,8 +225,13 @@
     for k in range(SIDE):
         norm[k * 8 : (k + 1) * 8, :] = from_second[1, k, 8:16, :].astype(jnp.bfloat16)
 
+    for copy in low_planes:
+        copy.wait()
+    low_copy = remote(lows.at[core], lows.at[core], small, 17, partner, y)
+    low_copy.start()
     arrive(2)
     send(5)
+    low_copy.wait()
     lane = lax.broadcasted_iota(jnp.int32, (48, 128), 1)
     unit = jnp.where(lax.broadcasted_iota(jnp.int32, (48, 128), 0) == lane, 1.0, 0.0).astype(jnp.bfloat16)
 
@@ -235,7 +241,7 @@
         x_at = minor + core_at * (major - minor)
         start = pl.multiple_of(index_of(z_at, x_at, core_at) * ROWS, ROWS)
         turned = lax.dot_general(
-            lows[core_at, k % 16], unit, (((0,), (0,)), ((), ())), preferred_element_type=jnp.float32
+            jnp.concatenate([lows[core_at, m, k % 16] for m in range(3)], axis=0), unit, (((0,), (0,)), ((), ())), preferred_element_type=jnp.float32
         )
         low_rows[pl.ds(start, ROWS), :] = turned.astype(jnp.bfloat16)
         return carry
@@ -316,66 +322,97 @@
     scale_mine(3)
     scale_mine_pair(6)
     scale_passed_pair(6)
-    arrive(8)
     sent(8)
     scale_mine(4)
+    arrive(8)
     scale_mine_pair(7)
     scale_passed_pair(7)
     arrive(9)
     sent(9)
-    scale_mine(5)
-    scale_mine_pair(8)
-    scale_passed_pair(8)
+    each_link(lambda link: pass_copy(link, 5).wait_send())
+    each_link(lambda link: pass_copy(link, 8).wait())
     each_link(lambda link: pass_copy(link, 9).wait())
+
+
+PARTLY = {
+    (2, 2): (),
+    (2, 1): ((1, 1),),
+    (1, 2): ((0, 1),),
+    (3, 2): ((0, 1), (1, 0), (1, 1)),
+    (2, 3): ((1, 1), (0, 0), (0, 1)),
+}
+LATE = 12
 
 
 def write_kernel(
     factors, inverse, norm, low_rows, mixes, full,
-    query, key, value, f_query, f_key, f_value, norm_out, late, sem,
+    query, key, value, f_query, f_key, f_value, norm_out, late, sem, late_sem, small_sem,
 ):
     zero = lax.axis_index("zero")
-    z, x = zero // 8, zero // 2 % 4
+    z, x, core = zero // 8, zero // 2 % 4, zero % 2
     outs = (query, key, value)
 
-    def start_of(k):
-        return pl.multiple_of(((z + 2 + k // 4) % 4 * 4 + (x + 2 + k % 4) % 4) * 2 * ROWS, 2 * ROWS)
-
-    def ready_copy(k, m):
-        rows = pl.ds(start_of(k), 2 * ROWS)
-        return pltpu.make_async_copy(full.at[m, rows, :], outs[m].at[rows, :], sem.at[k * 3 + m])
-
-    def late_copy(m):
-        return pltpu.make_async_copy(late.at[m], outs[m].at[pl.ds(start_of(0), 2 * ROWS), :], sem.at[m])
-
-    def start_ready(k, carry):
+    def start_of(dz, dx, half, other):
+        core_at = core + other * (1 - 2 * core)
+        return pl.multiple_of((((z + dz) % 4 * 4 + (x + dx) % 4) * 2 + core_at) * ROWS + half * 64, 64)
+
+    runs = []
+    for dz in range(4):
+        for dx in range(4):
+            if (dz, dx) not in PARTLY:
+                runs.append((pl.multiple_of(((z + dz) % 4 * 4 + (x + dx) % 4) * 2 * ROWS, 2 * ROWS), 2 * ROWS))
+    for (dz, dx), halves in PARTLY.items():
+        for half, other in halves:
+            runs.append((start_of(dz, dx, half, other), 64))
+    copies = []
+    for start, rows in runs:
         for m in range(3):
-            ready_copy(k, m).start()
-        return carry
-
-    def wait_ready(k, carry):
-        for m in range(3):
-            ready_copy(k, m).wait()
-        return carry
-
-    lax.fori_loop(1, 16, start_ready, 0)
-    for m, out in enumerate((f_query, f_key, f_value)):
-        out[...] = factors[m * 8 : (m + 1) * 8, :]
-    norm_out[...] = norm[...]
+            part = pl.ds(start, rows)
+            copies.append(pltpu.make_async_copy(full.at[m, part, :], outs[m].at[part, :], sem.at[len(copies)]))
+    copies += [
+        pltpu.make_async_copy(src, dst, small_sem.at[k])
+        for k, (src, dst) in enumerate(
+            (
+                (factors.at[pl.ds(0, 8), :], f_query), (factors.at[pl.ds(8, 8), :], f_key),
+                (factors.at[pl.ds(16, 8), :], f_value), (norm, norm_out),
+            )
+        )
+    ]
+    for copy in copies:
+        copy.start()
     scale = inverse[...]
+
+    def late_start(k):
+        group, half, turn = k // 4, k // 2 % 2, k % 2
+        is_0, is_1, is_2 = (2 - group) * (1 - group) // 2, group * (2 - group), group * (group - 1) // 2
+        side = 1 + 2 * turn
+        dz = is_0 * 2 + is_1 * (2 - half) + is_2 * ((1 - half) * side + half * 2)
+        dx = is_0 * 2 + is_1 * (1 + half) + is_2 * (half * side + (1 - half) * 2)
+        return start_of(dz, dx, half, (1 - is_2) * turn)
+
+    def late_copy(k, m):
+        return pltpu.make_async_copy(
+            late.at[k, m], outs[m].at[pl.ds(late_start(k), 64), :], late_sem.at[k * 3 + m]
+        )
 
     def scale_late(k, carry):
         def store(m, at, value):
-            late[m, pl.ds(pl.multiple_of(k * 64, 64), 64), at : at + 128] = value
-
-        scaled(low_rows, mixes, scale, 64, pl.multiple_of(start_of(0) + k * 64, 64), full, store)
+            late[k, m, :, at : at + 128] = value
+
+        scaled(low_rows, mixes, scale, 64, late_start(k), full, store)
+        for m in range(3):
+            late_copy(k, m).start()
         return carry
 
-    lax.fori_loop(0, 4, scale_late, 0)
-    for m in range(3):
-        late_copy(m).start()
-    lax.fori_loop(1, 16, wait_ready, 0)
-    for m in range(3):
-        late_copy(m).wait()
+    def wait_late(k, carry):
+        for m in range(3):
+            late_copy(k, m).wait()
+        return carry
+
+    lax.fori_loop(0, LATE, scale_late, 0)
+    for copy in copies:
+        copy.wait()
+    lax.fori_loop(0, LATE, wait_late, 0)
 
 
 def per_device(wq, lq, hq, wk, lk, hk, wv, lv, hv, train, step):
@@ -396,19 +433,21 @@
             pltpu.VMEM((3, 128, COLS), bf16),
             pltpu.VMEM((3, D_MODEL, COLS), bf16),
         ),
-        in_specs=[any_spec] * 9 + [vmem] * 2,
+        in_specs=[any_spec] * 11,
         out_specs=(vmem,) * 6,
         scratch_shapes=[
-            pltpu.VMEM((2, 16, 48, 128), bf16),
+            pltpu.VMEM((2, 1, 32), f32),
+            pltpu.VMEM((3, 16, 128), bf16),
+            pltpu.VMEM((2, 4, 16, 16, 128), bf16),
             pltpu.VMEM((3, 16, COLS), bf16),
             pltpu.VMEM((32, 128), f32),
             pltpu.VMEM((4, 8, 128), f32),
             pltpu.VMEM((32, 128), f32),
             pltpu.VMEM((4, 16, 128), f32),
             pltpu.VMEM((2, 4, 16, 128), f32),
-            pltpu.SemaphoreType.DMA((9,)),
-            pltpu.SemaphoreType.DMA((18,)),
-            pltpu.SemaphoreType.DMA((18,)),
+            pltpu.SemaphoreType.DMA((11,)),
+            pltpu.SemaphoreType.DMA((21,)),
+            pltpu.SemaphoreType.DMA((21,)),
             pltpu.SemaphoreType.DMA((N_MESSAGES * 4,)),
             pltpu.SemaphoreType.DMA((N_MESSAGES * 4,)),
             pltpu.SemaphoreType.DMA((N_MESSAGES * 4,)),
@@ -432,10 +471,12 @@
             jax.ShapeDtypeStruct((32, 128), bf16),
         ),
         in_specs=[vmem] * 6,
-        out_specs=[any_spec] * 3 + [vmem] * 4,
+        out_specs=[any_spec] * 7,
         scratch_shapes=[
-            pltpu.VMEM((3, 2 * ROWS, COLS), bf16),
-            pltpu.SemaphoreType.DMA((48,)),
+            pltpu.VMEM((LATE, 3, 64, COLS), bf16),
+            pltpu.SemaphoreType.DMA((57,)),
+            pltpu.SemaphoreType.DMA((LATE * 3,)),
+            pltpu.SemaphoreType.DMA((4,)),
         ],
         compiler_params=pltpu.CompilerParams(vmem_limit_bytes=WRITE_LIMIT * 1024 * 1024),
     )(*state)

time: 88.2 us -> 86.5 us (0.981)
  Pallas kernels: 87.4 us -> 85.7 us
    pallas_call x1, Pallas kernels: 78 us -> 76.5 us  [per_device(): pl.pallas_call(gather_kernel, out_shape=(jax.ShapeDtypeStruct((24, 128),...]
where the time goes in v4:
time: 86.5 us; the launch traced here: 86.4 us
  Pallas kernels  85.7 us (99%)
    pallas_call x1, Pallas kernels, per_device(): pl.pallas_call(gather_kernel, out_shape=(jax.ShapeDtypeStruct((24, 128),...  76.5 us
    pallas_call x1, Pallas kernels, per_device(): pl.pallas_call(write_kernel, out_shape=(jax.ShapeDtypeStruct((D_MODEL, CO...  9.18 us

profile of v4, /device:TPU:1, one launch (start us, length us, event | category | flops | bytes accessed | tf_op | source)
XLA Modules:
  0.0 86.4 jit_solution(549075147794346215)
XLA Ops:
  0.6 76.5 %shard_map.162 = (f32[24,128]{1,0:T(8,128)S(1)}, f32[24,128]{1,0:T(8,128)S(1)}, bf16[32,128]{1,0:T(8,128)(2,1)S(1)}, bf16[4096,128]{1,0:T(8,128)(2,1)S(1)}, bf16...) custom-call(bf16[128,1024]{1,0:T(8,128)(2,1)} %w_query.1, bf16[128,1024]{1,0:T(8,128)(2,1)} %w_key.1, ...), custom_call_target="tpu_custom_call" | custom-call | tf_op jit(solution)/shard_map/pallas_call | solution.py:426
  77.2 9.2 %shard_map.163 = (bf16[4096,1024]{1,0:T(8,128)(2,1)}, bf16[4096,1024]{1,0:T(8,128)(2,1)}, bf16[4096,1024]{1,0:T(8,128)(2,1)}, f32[8,128]{1,0:T(8,128)}, f32[8,12...) custom-call(f32[24,128]{1,0:T(8,128)S(1)} %get-tuple-element.20.factors, ...), custom_call_target="tpu_custom_call" | custom-call | tf_op jit(solution)/shard_map/pallas_call | solution.py:462

commit v5 on v4

--- a/solution.py
+++ b/solution.py
@@ -24,7 +24,8 @@
     (-1, 0, 1, 1, 0, 32),
     (-1, -1, 1, 1, 0, 32),
     (-1, 1, 1, 1, 0, 32),
-    (-1, 2, 1, 1, 0, 32),
+    (-1, 2, 1, 1, 0, 24),
+    (-1, 2, 1, 1, 24, 8),
 )
 N_MESSAGES = len(MESSAGES)
 
@@ -46,7 +47,7 @@
     w_query, w_key, w_value, low_query, low_key, low_value, high_query, high_key, high_value, train, step,
     factors, inverse, norm, low_rows, mixes, full,
     gains, low_own, lows, highs, message, from_y, from_core, from_first, from_second,
-    load_sem, small_send, small_recv, send_sem, recv_sem, pass_send, pass_recv, own_send, own_recv,
+    load_sem, small_send, small_recv, send_sem, recv_sem, pass_send, pass_recv, own_send, own_recv, near_sem, down_sem,
 ):
     zero, y = lax.axis_index("zero"), lax.axis_index("model")
     z, x, core = zero // 8, zero // 2 % 4, zero % 2
@@ -66,6 +67,29 @@
             src_ref=src, dst_ref=dst, send_sem=sems[0].at[at], recv_sem=sems[1].at[at],
             device_id=(target, y_at), device_id_type=MESH,
         )
+
+    def upstream(at, way):
+        return at // 2 if way == 1 else (at + 1) // 2 % 2
+
+    near = [
+        ((peer(0, 1), y), upstream(x, 1), 0), ((peer(0, 3), y), upstream(x, -1), 0),
+        ((peer(1, 1), y), upstream(z, 1), 1), ((peer(1, 3), y), upstream(z, -1), 1),
+        ((zero, (y + 1) % 4), upstream(y, 1), 2), ((zero, (y + 3) % 4), upstream(y, -1), 2),
+    ]
+    greeted = near + [((partner, y), 1 - core, 0)]
+    n_up = sum(up for _, up, _ in greeted)
+
+    def wait_down(group):
+        n_down = sum(1 - up for _, up, at in greeted if at == group)
+        pl.when(n_down > 0)(lambda: pl.semaphore_wait(down_sem.at[group], n_down))
+
+    barrier = pltpu.get_barrier_semaphore()
+
+    def signal(sem, device):
+        pl.semaphore_signal(sem, inc=1, device_id=device, device_id_type=MESH)
+
+    for device, up, _ in greeted:
+        pl.when(up == 0)(lambda device=device: signal(barrier, device))
 
     small = (small_send, small_recv)
     place = second * 4 + first
@@ -85,23 +109,18 @@
     for load in loads:
         load.start()
 
-    barrier = pltpu.get_barrier_semaphore()
-    pl.semaphore_signal(barrier, inc=1, device_id=(partner, y), device_id_type=MESH)
-    for k in range(1, SIDE):
-        pl.semaphore_signal(barrier, inc=1, device_id=(peer(0, k), y), device_id_type=MESH)
-        pl.semaphore_signal(barrier, inc=1, device_id=(peer(1, k), y), device_id_type=MESH)
-        pl.semaphore_signal(barrier, inc=1, device_id=(zero, (y + k) % 4), device_id_type=MESH)
-
     for load in loads[:2]:
         load.wait()
     gain = gains[0] + gains[1]
     gain = pltpu.roll(jnp.concatenate([gain, jnp.zeros((1, 96), jnp.float32)], axis=1), 32 * y, 1)
     row = lax.broadcasted_iota(jnp.int32, (8, 128), 0)
     tile = jnp.where(row == x * 2 + core, jnp.broadcast_to(gain, (8, 128)), 0.0)
-    from_y[pl.ds(y, 1)] = tile[None]
+    message[24:32, :] = tile
+    pl.when(n_up > 0)(lambda: pl.semaphore_wait(barrier, n_up))
+    for device, up, group in greeted:
+        pl.when(up == 1)(lambda device=device, group=group: signal(down_sem.at[group], device))
     for load in loads[2:5]:
         load.wait()
-    pl.semaphore_wait(barrier, 10)
 
     def rows_of(link, at, arriving, core_at):
         along, across, half, parts, skip, _ = MESSAGES[at]
@@ -143,12 +162,18 @@
 
         each_link(body)
 
-    send(0)
-    y_copies = [
-        remote(from_y.at[y], from_y.at[y], small, k, zero, (y + k) % 4) for k in range(1, SIDE)
-    ]
-    for copy in y_copies:
-        copy.start()
+    def send_first(to_up, axes):
+        def body(back):
+            for axis in axes:
+                at = (x, z)[axis]
+                up = (1 - back) * (at // 2) + back * ((at + 1) // 2 % 2)
+                pl.when(up == to_up)(lambda axis=axis: link_copy(2 * axis + back, 0).start())
+
+        each_link(body, 2)
+
+    send_first(1, (0, 1))
+    wait_down(0)
+    send_first(0, (0,))
 
     for load in loads[5:]:
         load.wait()
@@ -161,12 +186,15 @@
         total = jnp.sum(jnp.abs(value), axis=0, keepdims=True)
         for j in range(8):
             message[m * 8 + j : m * 8 + j + 1, :] = total[:, j * 128 : (j + 1) * 128]
-    for copy in y_copies:
-        copy.wait()
-    message[24:32, :] = from_y[0] + from_y[1] + from_y[2] + from_y[3]
 
     core_copy = remote(message, from_core, small, 0, partner, y)
     core_copy.start()
+    wait_down(1)
+    send_first(0, (1,))
+    wait_down(2)
+    for device, _, _ in near:
+        signal(near_sem, device)
+    pl.semaphore_wait(near_sem, 6)
     low_block = lows.at[core, y, place]
     low_first = [remote(low_block, low_block, small, 10 + k, peer(core, k), y) for k in range(1, SIDE)]
     for copy in low_first:
@@ -218,12 +246,19 @@
     for copy in low_planes:
         copy.start()
     sum_copy.wait()
+    from_y[pl.ds(y, 1)] = from_second[1, :, 8:16, :][None]
+    y_copies = [remote(from_y.at[y], from_y.at[y], small, k, zero, (y + k) % 4) for k in range(1, SIDE)]
+    for copy in y_copies:
+        copy.start()
     sums = [from_second[h, 0] + from_second[h, 1] + from_second[h, 2] + from_second[h, 3] for h in range(2)]
     factor = jnp.concatenate([sums[0], sums[1][:8]], axis=0) / D_MODEL
     factors[...] = factor
     inverse[...] = 1.0 / factor
+    for copy in y_copies:
+        copy.wait()
     for k in range(SIDE):
-        norm[k * 8 : (k + 1) * 8, :] = from_second[1, k, 8:16, :].astype(jnp.bfloat16)
+        rows = from_y[0, k] + from_y[1, k] + from_y[2, k] + from_y[3, k]
+        norm[k * 8 : (k + 1) * 8, :] = rows.astype(jnp.bfloat16)
 
     for copy in low_planes:
         copy.wait()
@@ -310,6 +345,7 @@
     scale_mine(0)
     arrive(5)
     send(9)
+    send(10)
     scale_passed(4)
     sent(5)
     scale_mine_pair(2)
@@ -328,10 +364,13 @@
     scale_mine_pair(7)
     scale_passed_pair(7)
     arrive(9)
+    arrive(10)
     sent(9)
+    sent(10)
     each_link(lambda link: pass_copy(link, 5).wait_send())
     each_link(lambda link: pass_copy(link, 8).wait())
     each_link(lambda link: pass_copy(link, 9).wait())
+    each_link(lambda link: pass_copy(link, 10).wait())
 
 
 PARTLY = {
@@ -441,7 +480,7 @@
             pltpu.VMEM((2, 4, 16, 16, 128), bf16),
             pltpu.VMEM((3, 16, COLS), bf16),
             pltpu.VMEM((32, 128), f32),
-            pltpu.VMEM((4, 8, 128), f32),
+            pltpu.VMEM((4, 4, 8, 128), f32),
             pltpu.VMEM((32, 128), f32),
             pltpu.VMEM((4, 16, 128), f32),
             pltpu.VMEM((2, 4, 16, 128), f32),
@@ -454,6 +493,8 @@
             pltpu.SemaphoreType.DMA((N_MESSAGES * 4,)),
             pltpu.SemaphoreType.DMA,
             pltpu.SemaphoreType.DMA,
+            pltpu.SemaphoreType.REGULAR,
+            pltpu.SemaphoreType.REGULAR((3,)),
         ],
         compiler_params=pltpu.CompilerParams(
             collective_id=0, has_side_effects=True, vmem_limit_bytes=GATHER_LIMIT * 1024 * 1024

time: 86.5 us -> 84.4 us (0.976)
  Pallas kernels: 85.7 us -> 83.7 us
    pallas_call x1, Pallas kernels: 76.5 us -> 74.5 us  [per_device(): pl.pallas_call(gather_kernel, out_shape=(jax.ShapeDtypeStruct((24, 128),...]
where the time goes in v5:
time: 84.4 us; the launch traced here: 84.3 us
  Pallas kernels  83.7 us (99%)
    pallas_call x1, Pallas kernels, per_device(): pl.pallas_call(gather_kernel, out_shape=(jax.ShapeDtypeStruct((24, 128),...  74.5 us
    pallas_call x1, Pallas kernels, per_device(): pl.pallas_call(write_kernel, out_shape=(jax.ShapeDtypeStruct((D_MODEL, CO...  9.18 us

profile of v5, /device:TPU:1, one launch (start us, length us, event | category | flops | bytes accessed | tf_op | source)
XLA Modules:
  0.0 84.3 jit_solution(17335395150590982366)
XLA Ops:
  0.6 74.5 %shard_map.162 = (f32[24,128]{1,0:T(8,128)S(1)}, f32[24,128]{1,0:T(8,128)S(1)}, bf16[32,128]{1,0:T(8,128)(2,1)S(1)}, bf16[4096,128]{1,0:T(8,128)(2,1)S(1)}, bf16...) custom-call(bf16[128,1024]{1,0:T(8,128)(2,1)} %w_query.1, bf16[128,1024]{1,0:T(8,128)(2,1)} %w_key.1, ...), custom_call_target="tpu_custom_call" | custom-call | tf_op jit(solution)/shard_map/pallas_call | solution.py:465
  75.1 9.2 %shard_map.163 = (bf16[4096,1024]{1,0:T(8,128)(2,1)}, bf16[4096,1024]{1,0:T(8,128)(2,1)}, bf16[4096,1024]{1,0:T(8,128)(2,1)}, f32[8,128]{1,0:T(8,128)}, f32[8,12...) custom-call(f32[24,128]{1,0:T(8,128)S(1)} %get-tuple-element.20.factors, ...), custom_call_target="tpu_custom_call" | custom-call | tf_op jit(solution)/shard_map/pallas_call | solution.py:503

commit v6 on v5

--- a/solution.py
+++ b/solution.py
@@ -10,6 +10,7 @@
 COLS = 1024
 ROWS = 128
 SUB = 32
+BLOCK = 64
 SIDE = 4
 GATHER_LIMIT = 16
 WRITE_LIMIT = 16
@@ -97,29 +98,24 @@
         pltpu.make_async_copy(src, dst, load_sem.at[k])
         for k, (src, dst) in enumerate(
             (
-                (train, gains.at[0]), (step, gains.at[1]),
                 (w_query, full.at[0, pl.ds(own, ROWS), :]),
                 (w_key, full.at[1, pl.ds(own, ROWS), :]),
                 (w_value, full.at[2, pl.ds(own, ROWS), :]),
                 (low_query, low_own.at[0]), (low_key, low_own.at[1]), (low_value, low_own.at[2]),
+                (train, gains.at[0]), (step, gains.at[1]),
                 (high_query, highs.at[0]), (high_key, highs.at[1]), (high_value, highs.at[2]),
             )
         )
     ]
-    for load in loads:
+    for load in loads[:3]:
         load.start()
 
-    for load in loads[:2]:
-        load.wait()
-    gain = gains[0] + gains[1]
-    gain = pltpu.roll(jnp.concatenate([gain, jnp.zeros((1, 96), jnp.float32)], axis=1), 32 * y, 1)
-    row = lax.broadcasted_iota(jnp.int32, (8, 128), 0)
-    tile = jnp.where(row == x * 2 + core, jnp.broadcast_to(gain, (8, 128)), 0.0)
-    message[24:32, :] = tile
     pl.when(n_up > 0)(lambda: pl.semaphore_wait(barrier, n_up))
     for device, up, group in greeted:
         pl.when(up == 1)(lambda device=device, group=group: signal(down_sem.at[group], device))
-    for load in loads[2:5]:
+    for load in loads[3:]:
+        load.start()
+    for load in loads[:3]:
         load.wait()
 
     def rows_of(link, at, arriving, core_at):
@@ -175,7 +171,15 @@
     wait_down(0)
     send_first(0, (0,))
 
-    for load in loads[5:]:
+    for load in loads[6:8]:
+        load.wait()
+    gain = gains[0] + gains[1]
+    gain = pltpu.roll(jnp.concatenate([gain, jnp.zeros((1, 96), jnp.float32)], axis=1), 32 * y, 1)
+    row = lax.broadcasted_iota(jnp.int32, (8, 128), 0)
+    tile = jnp.where(row == x * 2 + core, jnp.broadcast_to(gain, (8, 128)), 0.0)
+    message[24:32, :] = tile
+
+    for load in loads[3:6] + loads[8:]:
         load.wait()
     lows[core, y, place] = low_own[y - y // 3]
     for m in range(3):
@@ -352,7 +356,6 @@
     arrive(6)
     sent(6)
     scale_mine(1)
-    scale_passed(5)
     arrive(7)
     sent(7)
     scale_mine(3)
@@ -361,26 +364,17 @@
     sent(8)
     scale_mine(4)
     arrive(8)
-    scale_mine_pair(7)
-    scale_passed_pair(7)
     arrive(9)
     arrive(10)
     sent(9)
     sent(10)
-    each_link(lambda link: pass_copy(link, 5).wait_send())
-    each_link(lambda link: pass_copy(link, 8).wait())
+    for at in (5, 7, 8):
+        each_link(lambda link: pass_copy(link, at).wait())
     each_link(lambda link: pass_copy(link, 9).wait())
     each_link(lambda link: pass_copy(link, 10).wait())
 
 
-PARTLY = {
-    (2, 2): (),
-    (2, 1): ((1, 1),),
-    (1, 2): ((0, 1),),
-    (3, 2): ((0, 1), (1, 0), (1, 1)),
-    (2, 3): ((1, 1), (0, 0), (0, 1)),
-}
-LATE = 12
+LATE = ((2, 1), (1, 2), (3, 2), (2, 3), (2, 2))
 
 
 def write_kernel(
@@ -388,26 +382,21 @@
     query, key, value, f_query, f_key, f_value, norm_out, late, sem, late_sem, small_sem,
 ):
     zero = lax.axis_index("zero")
-    z, x, core = zero // 8, zero // 2 % 4, zero % 2
+    z, x = zero // 8, zero // 2 % 4
     outs = (query, key, value)
 
-    def start_of(dz, dx, half, other):
-        core_at = core + other * (1 - 2 * core)
-        return pl.multiple_of((((z + dz) % 4 * 4 + (x + dx) % 4) * 2 + core_at) * ROWS + half * 64, 64)
-
-    runs = []
+    def start_of(dz, dx):
+        return pl.multiple_of(((z + dz) % 4 * 4 + (x + dx) % 4) * 2 * ROWS, 2 * ROWS)
+
+    copies = []
     for dz in range(4):
         for dx in range(4):
-            if (dz, dx) not in PARTLY:
-                runs.append((pl.multiple_of(((z + dz) % 4 * 4 + (x + dx) % 4) * 2 * ROWS, 2 * ROWS), 2 * ROWS))
-    for (dz, dx), halves in PARTLY.items():
-        for half, other in halves:
-            runs.append((start_of(dz, dx, half, other), 64))
-    copies = []
-    for start, rows in runs:
-        for m in range(3):
-            part = pl.ds(start, rows)
-            copies.append(pltpu.make_async_copy(full.at[m, part, :], outs[m].at[part, :], sem.at[len(copies)]))
+            if (dz, dx) not in LATE:
+                for m in range(3):
+                    part = pl.ds(start_of(dz, dx), 2 * ROWS)
+                    copies.append(
+                        pltpu.make_async_copy(full.at[m, part, :], outs[m].at[part, :], sem.at[len(copies)])
+                    )
     copies += [
         pltpu.make_async_copy(src, dst, small_sem.at[k])
         for k, (src, dst) in enumerate(
@@ -422,23 +411,25 @@
     scale = inverse[...]
 
     def late_start(k):
-        group, half, turn = k // 4, k // 2 % 2, k % 2
-        is_0, is_1, is_2 = (2 - group) * (1 - group) // 2, group * (2 - group), group * (group - 1) // 2
-        side = 1 + 2 * turn
-        dz = is_0 * 2 + is_1 * (2 - half) + is_2 * ((1 - half) * side + half * 2)
-        dx = is_0 * 2 + is_1 * (1 + half) + is_2 * (half * side + (1 - half) * 2)
-        return start_of(dz, dx, half, (1 - is_2) * turn)
+        aside, along_z, way = 1 - k // 4, (k + 1) // 2 % 2, 2 * k - 3
+        return start_of(2 + aside * along_z * way, 2 + aside * (1 - along_z) * (way // 3))
 
     def late_copy(k, m):
         return pltpu.make_async_copy(
-            late.at[k, m], outs[m].at[pl.ds(late_start(k), 64), :], late_sem.at[k * 3 + m]
+            late.at[k, m], outs[m].at[pl.ds(late_start(k), 2 * ROWS), :], late_sem.at[k * 3 + m]
         )
 
     def scale_late(k, carry):
-        def store(m, at, value):
-            late[k, m, :, at : at + 128] = value
-
-        scaled(low_rows, mixes, scale, 64, late_start(k), full, store)
+        def scale_part(part, carry):
+            at_row = pl.multiple_of(part * BLOCK, BLOCK)
+
+            def store(m, at, value):
+                late[k, m, pl.ds(at_row, BLOCK), at : at + 128] = value
+
+            scaled(low_rows, mixes, scale, BLOCK, pl.multiple_of(late_start(k) + at_row, BLOCK), full, store)
+            return carry
+
+        lax.fori_loop(0, 2 * ROWS // BLOCK, scale_part, 0)
         for m in range(3):
             late_copy(k, m).start()
         return carry
@@ -448,10 +439,10 @@
             late_copy(k, m).wait()
         return carry
 
-    lax.fori_loop(0, LATE, scale_late, 0)
+    lax.fori_loop(0, len(LATE), scale_late, 0)
     for copy in copies:
         copy.wait()
-    lax.fori_loop(0, LATE, wait_late, 0)
+    lax.fori_loop(0, len(LATE), wait_late, 0)
 
 
 def per_device(wq, lq, hq, wk, lk, hk, wv, lv, hv, train, step):
@@ -514,9 +505,9 @@
         in_specs=[vmem] * 6,
         out_specs=[any_spec] * 7,
         scratch_shapes=[
-            pltpu.VMEM((LATE, 3, 64, COLS), bf16),
-            pltpu.SemaphoreType.DMA((57,)),
-            pltpu.SemaphoreType.DMA((LATE * 3,)),
+            pltpu.VMEM((len(LATE), 3, 2 * ROWS, COLS), bf16),
+            pltpu.SemaphoreType.DMA((33,)),
+            pltpu.SemaphoreType.DMA((len(LATE) * 3,)),
             pltpu.SemaphoreType.DMA((4,)),
         ],
         compiler_params=pltpu.CompilerParams(vmem_limit_bytes=WRITE_LIMIT * 1024 * 1024),

time: 84.4 us -> 84.1 us (level)
  no operation moved by 1% of the time
where the time goes in v6:
time: 84.1 us; the launch traced here: 83.9 us
  Pallas kernels  83.3 us (99%)
    pallas_call x1, Pallas kernels, per_device(): pl.pallas_call(gather_kernel, out_shape=(jax.ShapeDtypeStruct((24, 128),...  74.5 us
    pallas_call x1, Pallas kernels, per_device(): pl.pallas_call(write_kernel, out_shape=(jax.ShapeDtypeStruct((D_MODEL, CO...  8.82 us

profile of v6, /device:TPU:1, one launch (start us, length us, event | category | flops | bytes accessed | tf_op | source)
XLA Modules:
  0.0 83.9 jit_solution(2557017985797476245)
XLA Ops:
  0.6 74.5 %shard_map.162 = (f32[24,128]{1,0:T(8,128)S(1)}, f32[24,128]{1,0:T(8,128)S(1)}, bf16[32,128]{1,0:T(8,128)(2,1)S(1)}, bf16[4096,128]{1,0:T(8,128)(2,1)S(1)}, bf16...) custom-call(bf16[128,1024]{1,0:T(8,128)(2,1)} %w_query.1, bf16[128,1024]{1,0:T(8,128)(2,1)} %w_key.1, ...), custom_call_target="tpu_custom_call" | custom-call | tf_op jit(solution)/shard_map/pallas_call | solution.py:456
  75.1 8.8 %shard_map.163 = (bf16[4096,1024]{1,0:T(8,128)(2,1)}, bf16[4096,1024]{1,0:T(8,128)(2,1)}, bf16[4096,1024]{1,0:T(8,128)(2,1)}, f32[8,128]{1,0:T(8,128)}, f32[8,12...) custom-call(f32[24,128]{1,0:T(8,128)S(1)} %get-tuple-element.20.factors, ...), custom_call_target="tpu_custom_call" | custom-call | tf_op jit(solution)/shard_map/pallas_call | solution.py:494

commit v7 on v6

--- a/solution.py
+++ b/solution.py
@@ -170,6 +170,8 @@
     send_first(1, (0, 1))
     wait_down(0)
     send_first(0, (0,))
+    wait_down(1)
+    send_first(0, (1,))
 
     for load in loads[6:8]:
         load.wait()
@@ -193,8 +195,6 @@
 
     core_copy = remote(message, from_core, small, 0, partner, y)
     core_copy.start()
-    wait_down(1)
-    send_first(0, (1,))
     wait_down(2)
     for device, _, _ in near:
         signal(near_sem, device)

time: 84.1 us -> 84.1 us (level)
  no operation moved by 1% of the time
where the time goes in v7:
time: 84.1 us; the launch traced here: 83.9 us
  Pallas kernels  83.3 us (99%)
    pallas_call x1, Pallas kernels, per_device(): pl.pallas_call(gather_kernel, out_shape=(jax.ShapeDtypeStruct((24, 128),...  74.5 us
    pallas_call x1, Pallas kernels, per_device(): pl.pallas_call(write_kernel, out_shape=(jax.ShapeDtypeStruct((D_MODEL, CO...  8.82 us

profile of v7, /device:TPU:1, one launch (start us, length us, event | category | flops | bytes accessed | tf_op | source)
XLA Modules:
  0.0 83.9 jit_solution(4014404644604361016)
XLA Ops:
  0.6 74.5 %shard_map.162 = (f32[24,128]{1,0:T(8,128)S(1)}, f32[24,128]{1,0:T(8,128)S(1)}, bf16[32,128]{1,0:T(8,128)(2,1)S(1)}, bf16[4096,128]{1,0:T(8,128)(2,1)S(1)}, bf16...) custom-call(bf16[128,1024]{1,0:T(8,128)(2,1)} %w_query.1, bf16[128,1024]{1,0:T(8,128)(2,1)} %w_key.1, ...), custom_call_target="tpu_custom_call" | custom-call | tf_op jit(solution)/shard_map/pallas_call | solution.py:456
  75.1 8.8 %shard_map.163 = (bf16[4096,1024]{1,0:T(8,128)(2,1)}, bf16[4096,1024]{1,0:T(8,128)(2,1)}, bf16[4096,1024]{1,0:T(8,128)(2,1)}, f32[8,128]{1,0:T(8,128)}, f32[8,12...) custom-call(f32[24,128]{1,0:T(8,128)S(1)} %get-tuple-element.20.factors, ...), custom_call_target="tpu_custom_call" | custom-call | tf_op jit(solution)/shard_map/pallas_call | solution.py:494

commit v8 on v7

--- a/solution.py
+++ b/solution.py
@@ -156,7 +156,11 @@
             link_copy(link, at, 1).wait_recv()
             pass_copy(link, at).start()
 
-        each_link(body)
+        if at < 9:
+            each_link(body)
+        else:
+            for link in range(4):
+                body(link)
 
     def send_first(to_up, axes):
         def body(back):
@@ -364,12 +368,12 @@
     sent(8)
     scale_mine(4)
     arrive(8)
+    for at in (5, 7, 8):
+        each_link(lambda link: pass_copy(link, at).wait())
     arrive(9)
     arrive(10)
     sent(9)
     sent(10)
-    for at in (5, 7, 8):
-        each_link(lambda link: pass_copy(link, at).wait())
     each_link(lambda link: pass_copy(link, 9).wait())
     each_link(lambda link: pass_copy(link, 10).wait())
 

time: 84.1 us -> 84.1 us (level)
  no operation moved by 1% of the time
where the time goes in v8:
time: 84.1 us; the launch traced here: 83.9 us
  Pallas kernels  83.3 us (99%)
    pallas_call x1, Pallas kernels, per_device(): pl.pallas_call(gather_kernel, out_shape=(jax.ShapeDtypeStruct((24, 128),...  74.5 us
    pallas_call x1, Pallas kernels, per_device(): pl.pallas_call(write_kernel, out_shape=(jax.ShapeDtypeStruct((D_MODEL, CO...  8.82 us

profile of v8, /device:TPU:1, one launch (start us, length us, event | category | flops | bytes accessed | tf_op | source)
XLA Modules:
  0.0 83.9 jit_solution(10491622126591249181)
XLA Ops:
  0.6 74.5 %shard_map.162 = (f32[24,128]{1,0:T(8,128)S(1)}, f32[24,128]{1,0:T(8,128)S(1)}, bf16[32,128]{1,0:T(8,128)(2,1)S(1)}, bf16[4096,128]{1,0:T(8,128)(2,1)S(1)}, bf16...) custom-call(bf16[128,1024]{1,0:T(8,128)(2,1)} %w_query.1, bf16[128,1024]{1,0:T(8,128)(2,1)} %w_key.1, ...), custom_call_target="tpu_custom_call" | custom-call | tf_op jit(solution)/shard_map/pallas_call | solution.py:460
  75.1 8.8 %shard_map.163 = (bf16[4096,1024]{1,0:T(8,128)(2,1)}, bf16[4096,1024]{1,0:T(8,128)(2,1)}, bf16[4096,1024]{1,0:T(8,128)(2,1)}, f32[8,128]{1,0:T(8,128)}, f32[8,12...) custom-call(f32[24,128]{1,0:T(8,128)S(1)} %get-tuple-element.20.factors, ...), custom_call_target="tpu_custom_call" | custom-call | tf_op jit(solution)/shard_map/pallas_call | solution.py:498
